TPU v7x, 64 devices: a 2x2x8 block of a 4x4x8 slice. The times are simulated.
64 devices in a mesh: rep: 8 (over x, y, core), dp: 8 (over z).
Axes of the slice: x: 2, y: 2, z: 8, core: 2. Of those that a mesh axis runs over, the one named last changes fastest.
The devices are a block of a 4x4x8 slice.
Arguments:
- x: bfloat16 [64, 2048, 640], P(('rep', 'dp')), parts along dimension 0
- dy: bfloat16 [64, 2048, 640], P(('rep', 'dp')), parts along dimension 0
- w_gate: bfloat16 [2, 640, 2048], replicated
- w_up: bfloat16 [2, 640, 2048], replicated
- w_down: bfloat16 [2, 2048, 640], replicated
- m_w_gate: float32 [2, 640, 2048], replicated
- m_w_up: float32 [2, 640, 2048], replicated
- m_w_down: float32 [2, 2048, 640], replicated
- v_w_gate: float32 [2, 640, 2048], replicated
- v_w_up: float32 [2, 640, 2048], replicated
- v_w_down: float32 [2, 2048, 640], replicated
Outputs:
- output 1: bfloat16 [16, 640, 2048], P('rep'), parts along dimension 0
- output 2: bfloat16 [16, 640, 2048], P('rep'), parts along dimension 0
- output 3: bfloat16 [16, 2048, 640], P('rep'), parts along dimension 0
- output 4: float32 [16, 640, 2048], P('rep'), parts along dimension 0
- output 5: float32 [16, 640, 2048], P('rep'), parts along dimension 0
- output 6: float32 [16, 2048, 640], P('rep'), parts along dimension 0
- output 7: float32 [16, 640, 2048], P('rep'), parts along dimension 0
- output 8: float32 [16, 640, 2048], P('rep'), parts along dimension 0
- output 9: float32 [16, 2048, 640], P('rep'), parts along dimension 0
There are 8 independent parts. A program takes and returns all parts, laid end to end along the dimension named above; an argument that names none is the same for every part.
All inputs are finite; a program needn't handle non-finite values.
Results may differ from a plain program's by a relative error of at most 0.022.
Values are sent between devices in bfloat16 or wider.
A program may use at most 768 MiB of HBM per device.

v0:
```python
import jax
import jax.numpy as jnp
from jax import lax
from jax.sharding import PartitionSpec as P

NAMES = ("w_gate", "w_up", "w_down")


def matmul(a, w):
    return jnp.dot(a, w, preferred_element_type=jnp.float32).astype(jnp.bfloat16)


def normed(h):
    wide = h.astype(jnp.float32)
    scale = lax.rsqrt(jnp.mean(wide**2, -1, keepdims=True) + 1e-6)
    return (wide * scale).astype(jnp.bfloat16)


def layer(h, w):
    a = normed(h)
    gate = jnp.dot(a, w["w_gate"], preferred_element_type=jnp.float32)
    up = jnp.dot(a, w["w_up"], preferred_element_type=jnp.float32)
    return h + matmul((jax.nn.silu(gate) * up).astype(jnp.bfloat16), w["w_down"])


def adamw(w, m, v, g):
    m = 0.9 * m + 0.1 * g
    v = 0.95 * v + 0.05 * g * g
    step = m * lax.rsqrt(v + 1e-8) + 0.1 * w
    return (w - 0.02 * step).astype(jnp.bfloat16), m, v


def solution(mesh):
    def step(x, dy, *arrays):
        weights, m, v = (arrays[i : i + 3] for i in (0, 3, 6))
        layers = weights[0].shape[0]
        h, kept = x[0], []
        for number in range(layers):
            kept.append(h)
            h = layer(h, {name: w[number] for name, w in zip(NAMES, weights, strict=True)})
        by_h, summed = dy[0], [None] * layers
        for number in reversed(range(layers)):
            _, back = jax.vjp(lambda w, h: layer(h, w), {name: w[number] for name, w in zip(NAMES, weights, strict=True)}, kept[number])
            by_w, by_h = back(by_h)
            summed[number] = [lax.psum(by_w[name], "dp") for name in NAMES]
        gradients = [jnp.stack([summed[number][i] for number in range(layers)]).astype(jnp.float32) for i in range(3)]
        new = [adamw(w.astype(jnp.float32), m, v, g) for w, m, v, g in zip(weights, m, v, gradients, strict=True)]
        return tuple(one[which] for which in range(3) for one in new)

    return jax.shard_map(
        step,
        mesh=mesh,
        in_specs=(P(("rep", "dp"), None, None),) * 2 + (P(None, None, None),) * 9,
        out_specs=(P("rep", None, None),) * 9,
        check_vma=False,
    )
```

profile of v0, /device:TPU:22, one launch (start us, length us, event | category | flops | bytes accessed | tf_op | source)
XLA Modules:
  0.0 606.3 jit_solution(17771481322356062846)
XLA Ops:
  7.2 0.1 all-reduce.3.cloned.1.call-start
  7.3 3.0 copy.20
  10.3 0.6 fusion.30
  10.8 4.7 copy.21
  15.6 11.3 %convolution_convert_fusion.1 = bf16[2048,2048]{1,0:T(8,128)(2,1)} fusion(bf16[1,2048,640]{2,1,0:T(8,128)(2,1)} %param.12, bf16[2,2048,640]{2,1,0:T(8,128)(2,1)} %param.15), kind=kOutput, calls=%fused_computation.56 | convolution fusion | flops 5372903424 | bytes 13631488 | tf_op jit(solution)/shard_map/transpose(jvp())/dot_general | solution.py:10
  26.8 11.6 %fusion.68 = f32[2048,2048]{1,0:T(8,128)} fusion(bf16[2,640,2048]{2,1,0:T(8,128)(2,1)} %param.13, bf16[1,2048,640]{2,1,0:T(8,128)(2,1)S(1)} %copy-done.5, f32[2048]{0:T(1024)S(1)} %add_rsqrt_fusion), kind=kOutput, calls=%fused_computation.101 | convolution fusion | flops 5372641280 | bytes 22028288 | tf_op jit(solution)/shard_map/dot_general | solution.py:21
  38.4 16.9 %multiply_convert_fusion.1 = (bf16[2048,2048]{1,0:T(8,128)(2,1)}, f32[2048,2048]{1,0:T(8,128)}) fusion(f32[2048,2048]{1,0:T(8,128)} %fusion.68, bf16[2,640,2048]{2,1,0:T(8,128)(2,1)} %param.14, bf16[1,2048,640]{2,1,0:T(8,128)(2,1)} %param.11, f32[2048]{0:T(1024)S(1)} %add_rsqrt_fusion), kind=kOutput, calls=%fused_computation.17 | convolution fusion | flops 5397807104 | bytes 47194112 | tf_op jit(solution)/shard_map/dot_general | solution.py:22
  55.3 9.2 %fusion.34 = (f32[2048]{0:T(1024)S(1)}, bf16[2048,640]{0,1:T(8,128)(2,1)S(1)}) fusion(bf16[2048,2048]{1,0:T(8,128)(2,1)} %get-tuple-element.24, bf16[2,2048,640]{2,1,0:T(8,128)(2,1)} %param.15, bf16[1,2048,640]{1,2,0:T(8,128)(2,1)S(1)} %copy.20), kind=kOutput, calls=%fused_computation.64 | convolution fusion | flops 5375260672 | bytes 16261120 | tf_op jit(solution)/shard_map/dot_general | solution.py:10
  64.5 1.5 copy-done.3
  66.0 12.2 %fusion.57 = f32[2048,2048]{1,0:T(8,128)} fusion(bf16[2,640,2048]{2,1,0:T(8,128)(2,1)} %param.14, bf16[2048,640]{0,1:T(8,128)(2,1)S(1)} %get-tuple-element.27, f32[2048]{0:T(1024)S(1)} %fusion.92), kind=kOutput, calls=%fused_computation.90 | convolution fusion | flops 5372641280 | bytes 22028288 | tf_op jit(solution)/shard_map/jvp()/dot_general | solution.py:22
  78.1 25.1 %fusion.2 = (bf16[2048,2048]{1,0:T(8,128)(2,1)}, f32[2048,2048]{1,0:T(8,128)}) fusion(f32[2048,2048]{1,0:T(8,128)} %fusion.57, bf16[2048,2048]{1,0:T(8,128)(2,1)} %convolution_convert_fusion.1, bf16[2,640,2048]{2,1,0:T(8,128)(2,1)} %param.13, bf16[2048,640]{0,1:T(8,128)(2,1)} %copy-done.3, f32[2048]{0:T(1024)S(1)} %fusion.92), kind=kOutput, calls=%fused_computation.8 | convolution fusion | flops 5422972928 | bytes 55582720 | tf_op jit(solution)/shard_map/jvp()/dot_general | solution.py:21
  103.3 16.9 %fusion.49 = bf16[1,2048,640]{2,1,0:T(8,128)(2,1)} fusion(f32[2048,2048]{1,0:T(8,128)} %fusion.57, bf16[1,2048,640]{2,1,0:T(8,128)(2,1)} %param.12, f32[2048,2048]{1,0:T(8,128)} %get-tuple-element.29), kind=kOutput, calls=%fused_computation.82 | convolution fusion | flops 5395185664 | bytes 38797312 | tf_op jit(solution)/shard_map/transpose(jvp())/dot_general | solution.py:10
  120.2 13.3 %fusion.52 = bf16[1,640,2048]{2,1,0:T(8,128)(2,1)} fusion(bf16[2048,2048]{1,0:T(8,128)(2,1)} %convolution_convert_fusion.1, bf16[2048,640]{0,1:T(8,128)(2,1)} %copy-done.3, f32[2048]{0:T(1024)S(1)} %fusion.92, f32[2048,2048]{1,0:T(8,128)} %get-tuple-element.29), kind=kOutput, calls=%fused_computation.85 | convolution fusion | flops 5399117824 | bytes 30416896 | tf_op jit(solution)/shard_map/transpose(jvp())/dot_general | solution.py:22
  133.5 12.4 %fusion.38 = bf16[2048,640]{0,1:T(8,128)(2,1)} fusion(bf16[2048,2048]{1,0:T(8,128)(2,1)} %convolution_convert_fusion.1, bf16[2,640,2048]{2,1,0:T(8,128)(2,1)S(1)} %bitcast.77, f32[2048,2048]{1,0:T(8,128)} %get-tuple-element.29), kind=kOutput, calls=%fused_computation.72 | convolution fusion | flops 5395185664 | bytes 30408704 | tf_op jit(solution)/shard_map/transpose(jvp())/dot_general | solution.py:22
  145.9 10.9 %fusion.50 = bf16[1,640,2048]{2,1,0:T(8,128)(2,1)} fusion(bf16[2048,2048]{1,0:T(8,128)(2,1)} %get-tuple-element.28, bf16[2048,640]{0,1:T(8,128)(2,1)} %copy-done.3, f32[2048]{0:T(1024)S(1)} %fusion.92), kind=kOutput, calls=%fused_computation.83 | convolution fusion | flops 5372641280 | bytes 13639680 | tf_op jit(solution)/shard_map/transpose(jvp())/dot_general | solution.py:21
  156.9 8.5 %fusion.36 = (f32[2048]{0:T(1024)S(1)}, bf16[2048,640]{0,1:T(8,128)(2,1)S(1)}) fusion(bf16[2048,640]{0,1:T(8,128)(2,1)S(1)} %copy-done.4, bf16[2048,640]{0,1:T(8,128)(2,1)S(1)} %copy-done.12, bf16[2048,2048]{1,0:T(8,128)(2,1)} %get-tuple-element.28, bf16[2,640,2048]{2,1,0:T(8,128)(2,1)S(1)} %bitcast.75), kind=kOutput, calls=%fused_computation.66 | convolution fusion | flops 5375260672 | bytes 18882560 | tf_op jit(solution)/shard_map/transpose(jvp())/dot_general | solution.py:21
  165.4 2.0 fusion.54
  167.5 10.5 %fusion.51 = bf16[1,2048,640]{2,1,0:T(8,128)(2,1)} fusion(bf16[2048,2048]{1,0:T(8,128)(2,1)} %get-tuple-element.24, bf16[2048,640]{0,1:T(8,128)(2,1)S(1)} %fusion.54), kind=kOutput, calls=%fused_computation.84 | convolution fusion | flops 5370019840 | bytes 13631488 | tf_op jit(solution)/shard_map/transpose(jvp())/dot_general | solution.py:10
  178.0 7.3 %convolution_convert_fusion = bf16[2048,2048]{1,0:T(8,128)(2,1)S(1)} fusion(bf16[2048,640]{0,1:T(8,128)(2,1)S(1)} %fusion.54, bf16[2,2048,640]{2,1,0:T(8,128)(2,1)S(1)} %bitcast.79), kind=kOutput, calls=%fused_computation.55 | convolution fusion | flops 5372903424 | bytes 13631488 | tf_op jit(solution)/shard_map/transpose(jvp())/dot_general | solution.py:10
  185.3 13.9 %fusion.45 = bf16[1,640,2048]{2,1,0:T(8,128)(2,1)} fusion(bf16[2048,2048]{1,0:T(8,128)(2,1)S(1)} %convolution_convert_fusion, f32[2048,2048]{1,0:T(8,128)} %fusion.68, bf16[1,2048,640]{1,2,0:T(8,128)(2,1)S(1)} %copy-done.2, f32[2048]{0:T(1024)S(1)} %copy-done.10), kind=kOutput, calls=%fused_computation.80 | convolution fusion | flops 5399117824 | bytes 30416896 | tf_op jit(solution)/shard_map/transpose(jvp())/dot_general | solution.py:22
  199.2 19.0 %fusion.46 = bf16[1,640,2048]{2,1,0:T(8,128)(2,1)} fusion(f32[2048,2048]{1,0:T(8,128)} %fusion.68, f32[2048,2048]{1,0:T(8,128)} %get-tuple-element.25, bf16[2048,2048]{1,0:T(8,128)(2,1)} %copy-done.11, bf16[1,2048,640]{1,2,0:T(8,128)(2,1)S(1)} %copy-done.2, f32[2048]{0:T(1024)S(1)} %copy-done.10), kind=kOutput, calls=%fused_computation.81 | convolution fusion | flops 5420089344 | bytes 47194112 | tf_op jit(solution)/shard_map/transpose(jvp())/dot_general | solution.py:21
  218.3 323.5 %all-reduce.3.cloned.1.call-done = (bf16[1,640,2048]{2,1,0:T(8,128)(2,1)}, bf16[1,640,2048]{2,1,0:T(8,128)(2,1)}, bf16[1,640,2048]{2,1,0:T(8,128)(2,1)}, bf16[1,...) async-done(((bf16[1,640,2048]{2,1,0:T(8,128)(2,1)}, bf16[1,640,2048]{2,1,0:T(8,128)(2,1)}, bf16[1,640,2048]{2,1,0:T(8,128)(2,1)}, ...) | async-done | bytes 15728656 | tf_op jit(solution)/shard_map/psum | solution.py:45
  541.8 22.1 %fusion.23 = (bf16[2,2048,640]{2,1,0:T(8,128)(2,1)}, f32[2,2048,640]{2,1,0:T(8,128)}, f32[2,2048,640]{2,1,0:T(8,128)}) fusion(bf16[2,2048,640]{2,1,0:T(8,128)(2,1)} %param.15, bf16[1,2048,640]{2,1,0:T(8,128)(2,1)} %get-tuple-element.13, bf16[1,2048,640]{2,1,0:T(8,128)(2,1)} %get-tuple-element.14, f32[2,2048,640]{2,1,0:T(8,128)} %param.21, ...), kind=kLoop, calls=%fused_computation.44 | loop fusion | flops 49807360 | bytes 57671680 | tf_op jit(solution)/shard_map/convert_element_type | solution.py:30
  563.9 35.1 %fusion.15 = (bf16[2,640,2048]{2,1,0:T(8,128)(2,1)}, f32[2,640,2048]{2,1,0:T(8,128)}, f32[2,640,2048]{2,1,0:T(8,128)}, bf16[2,640,2048]{2,1,0:T(8,128)(2,1)}, f3...) fusion(bf16[2,640,2048]{2,1,0:T(8,128)(2,1)} %param.13, bf16[1,640,2048]{2,1,0:T(8,128)(2,1)S(1)} %copy-done.6, ...), kind=kLoop, calls=%fused_computation.36 | loop fusion | flops 99614720 | bytes 115343360 | tf_op jit(solution)/shard_map/convert_element_type | solution.py:30
  (44 shorter events, 0.2 us)
Async XLA Ops:
  7.2 534.6 %all-reduce.3.cloned.1.call-start = ((), (), s32[]{:S(2)}) async-start(), calls=%async_computation | async-start | bytes 31457280 | tf_op jit(solution)/shard_map/psum | solution.py:45
  10.3 45.0 %copy-start.1 = (bf16[1,2048,640]{1,2,0:T(8,128)(2,1)}, bf16[1,2048,640]{1,2,0:T(8,128)(2,1)S(1)}, u32[]{:S(2)}) copy-start(bf16[1,2048,640]{1,2,0:T(8,128)(2,1)S(1)} %copy.20) | copy-start | bytes 7864324
  10.8 27.6 %copy-start.9 = (f32[2048]{0:T(1024)}, f32[2048]{0:T(1024)S(1)}, u32[]{:S(2)}) copy-start(f32[2048]{0:T(1024)S(1)} %add_rsqrt_fusion) | copy-start | bytes 24580
  15.6 11.3 %copy-start.5 = (bf16[1,2048,640]{2,1,0:T(8,128)(2,1)S(1)}, bf16[1,2048,640]{2,1,0:T(8,128)(2,1)}, u32[]{:S(2)}) copy-start(bf16[1,2048,640]{2,1,0:T(8,128)(2,1)} %param.11) | copy-start | bytes 7864324
  64.5 1.5 copy-start.3
  64.5 1.5 copy-start.7
  78.1 55.4 %slice-start.2 = ((s8[5242880]{0:T(1024)(128)(4,1)}), s8[1048576]{0:T(1024)(128)(4,1)S(1)}, s32[]{:S(2)}) async-start(s8[5242880]{0:T(1024)(128)(4,1)} %bitcast.76), calls=%async_computation.3 | async-start | bytes 2097152
  103.3 30.2 %slice-start.3 = ((s8[5242880]{0:T(1024)(128)(4,1)}), s8[4194304]{0:T(1024)(128)(4,1)S(1)}, s32[]{:S(2)}) async-start(s8[5242880]{0:T(1024)(128)(4,1)} %bitcast.76), calls=%async_computation.4 | async-start | bytes 8388608
  120.2 36.7 %slice-start = ((s8[5242880]{0:T(1024)(128)(4,1)}), s8[4194304]{0:T(1024)(128)(4,1)S(1)}, s32[]{:S(2)}) async-start(s8[5242880]{0:T(1024)(128)(4,1)} %bitcast.74), calls=%async_computation.1 | async-start | bytes 8388608
  133.5 23.3 %slice-start.1 = ((s8[5242880]{0:T(1024)(128)(4,1)}), s8[1048576]{0:T(1024)(128)(4,1)S(1)}, s32[]{:S(2)}) async-start(s8[5242880]{0:T(1024)(128)(4,1)} %bitcast.74), calls=%async_computation.2 | async-start | bytes 2097152
  145.9 10.9 %copy-start.4 = (bf16[2048,640]{0,1:T(8,128)(2,1)S(1)}, bf16[2048,640]{0,1:T(8,128)(2,1)}, u32[]{:S(2)}) copy-start(bf16[2048,640]{0,1:T(8,128)(2,1)} %copy-done.3) | copy-start | bytes 7864324
  145.9 10.9 %copy-start.12 = (bf16[2048,640]{0,1:T(8,128)(2,1)S(1)}, bf16[2048,640]{0,1:T(8,128)(2,1)}, u32[]{:S(2)}) copy-start(bf16[2048,640]{0,1:T(8,128)(2,1)} %fusion.38) | copy-start | bytes 7864324
  156.9 8.5 %copy-start.8 = (f32[2048]{0:T(1024)S(1)}, f32[2048]{0:T(1024)}, u32[]{:S(2)}) copy-start(f32[2048]{0:T(1024)} %copy-done.7) | copy-start | bytes 24580
  156.9 8.5 %copy-start = (bf16[1,2048,640]{1,2,0:T(8,128)(2,1)S(1)}, bf16[1,2048,640]{1,2,0:T(8,128)(2,1)}, u32[]{:S(2)}) copy-start(bf16[1,2048,640]{1,2,0:T(8,128)(2,1)} %copy.21) | copy-start | bytes 7864324
  165.4 12.5 %slice-start.4 = ((s8[5242880]{0:T(1024)(128)(4,1)}), s8[1048576]{0:T(1024)(128)(4,1)S(1)}, s32[]{:S(2)}) async-start(s8[5242880]{0:T(1024)(128)(4,1)} %bitcast.78), calls=%async_computation.5 | async-start | bytes 2097152
  167.5 10.5 %slice-start.5 = ((s8[5242880]{0:T(1024)(128)(4,1)}), s8[4194304]{0:T(1024)(128)(4,1)S(1)}, s32[]{:S(2)}) async-start(s8[5242880]{0:T(1024)(128)(4,1)} %bitcast.78), calls=%async_computation.6 | async-start | bytes 8388608
  178.0 7.3 %copy-start.2 = (bf16[1,2048,640]{1,2,0:T(8,128)(2,1)S(1)}, bf16[1,2048,640]{1,2,0:T(8,128)(2,1)}, u32[]{:S(2)}) copy-start(bf16[1,2048,640]{1,2,0:T(8,128)(2,1)} %copy-done.1) | copy-start | bytes 7864324
  178.0 7.3 %copy-start.10 = (f32[2048]{0:T(1024)S(1)}, f32[2048]{0:T(1024)}, u32[]{:S(2)}) copy-start(f32[2048]{0:T(1024)} %copy-done.9) | copy-start | bytes 24580
  185.3 13.9 %copy-start.11 = (bf16[2048,2048]{1,0:T(8,128)(2,1)}, bf16[2048,2048]{1,0:T(8,128)(2,1)S(1)}, u32[]{:S(2)}) copy-start(bf16[2048,2048]{1,0:T(8,128)(2,1)S(1)} %convolution_convert_fusion) | copy-start | bytes 25165828
  541.8 22.1 %copy-start.6 = (bf16[1,640,2048]{2,1,0:T(8,128)(2,1)S(1)}, bf16[1,640,2048]{2,1,0:T(8,128)(2,1)}, u32[]{:S(2)}) copy-start(bf16[1,640,2048]{2,1,0:T(8,128)(2,1)} %get-tuple-element.9) | copy-start | bytes 7864324
Sparse Core Ops, SparseCore 0:
  218.4 323.3 all-reduce.2
where the time goes:
time: 616 us; the launch traced here: 606 us
  waiting for transfers between devices  324 us (53%)
  matrix products  199 us (32%)
  other arithmetic  59.8 us (10%)
  between operations  14.8 us (2%)
  local copies, waits for them, and re-layouts  9.26 us (2%)
    psum x1, waiting for transfers between devices, step(): summed[number] = [lax.psum(by_w[name], 'dp') for name in NAMES]  324 us
    dot_general x5, matrix products, layer(): gate = jnp.dot(a, w['w_gate'], preferred_element_type=jnp.float32)  75.1 us
    dot_general x5, matrix products, layer(): up = jnp.dot(a, w['w_up'], preferred_element_type=jnp.float32)  68.7 us
    convert_element_type x2, other arithmetic, adamw(): return ((w - 0.02 * step).astype(jnp.bfloat16), m, v)  57.1 us
    dot_general x5, matrix products, matmul(): jnp.dot(a, w, preferred_element_type=jnp.float32).astype(jnp.bfloat16)  55.1 us
  transfers between devices with their start and end apart: 1, of which 1 were waited for; matrix products, arithmetic and copies ran while one was open for 0% of the time, Pallas kernels for 0%

commit v1 on v0

v1 whole, which is shorter than its diff:
```python
import functools

import jax
import jax.numpy as jnp
from jax import lax
from jax.experimental import pallas as pl
from jax.experimental.pallas import tpu as pltpu
from jax.sharding import PartitionSpec as P

F32, BF16 = jnp.float32, jnp.bfloat16
LANES = 128
TILE = 256
SLOTS = 6
GAP = 2


def dot(a, b):
    return jnp.dot(a, b, preferred_element_type=F32)


def dot_t(a, b):
    return lax.dot_general(a, b, (((1,), (1,)), ((), ())), preferred_element_type=F32)


def scale_of(wide):
    return lax.rsqrt(jnp.mean(wide * wide, -1, keepdims=True) + 1e-6)


class Sizes:
    def __init__(self, mesh, x, w_gate):
        self.n = mesh.shape["dp"]
        self.tokens, self.d = x.shape[1:]
        self.layers, _, self.ff = w_gate.shape
        self.units = self.ff // TILE
        self.rows = self.d // self.n
        self.down = TILE // 2 // self.n
        self.halves, self.fifths = TILE // LANES, self.d // LANES
        self.message = self.halves * self.rows + self.fifths * self.down


def step_kernel(s, x_hbm, dy_hbm, wg_hbm, wu_hbm, wd_hbm, *refs):
    (own_x, own_y), refs = (refs[0:2], refs[2:4]), refs[4:]
    (wg, wu, wd, xh, a, a_t, dh, dh_t, dg, du, hid, own, got, final, gs, us, ds, hs, ps) = refs[:19]
    (load_sem, w_sem, send_sem, recv_sem, out_sem) = refs[19:]
    me = lax.axis_index("dp")
    right, left = lax.rem(me + 1, s.n), lax.rem(me + s.n - 1, s.n)
    towards = (right, left)

    barrier = pltpu.get_barrier_semaphore()
    for neighbour in towards:
        pl.semaphore_signal(barrier, inc=1, device_id={"dp": neighbour}, device_id_type=pl.DeviceIdType.MESH)

    first = [
        pltpu.make_async_copy(x_hbm.at[0], xh, load_sem.at[0]),
        pltpu.make_async_copy(wg_hbm.at[0], dg.at[pl.ds(0, s.d)], load_sem.at[1]),
        pltpu.make_async_copy(wu_hbm.at[0], dg.at[pl.ds(s.d, s.d)], load_sem.at[2]),
        pltpu.make_async_copy(wd_hbm.at[0], du.at[:, pl.ds(0, s.d)], load_sem.at[3]),
    ]
    second = [
        pltpu.make_async_copy(dy_hbm.at[0], dh, load_sem.at[4]),
        pltpu.make_async_copy(wg_hbm.at[1], wg, load_sem.at[5]),
        pltpu.make_async_copy(wu_hbm.at[1], wu, load_sem.at[6]),
        pltpu.make_async_copy(wd_hbm.at[1], wd, load_sem.at[7]),
    ]
    for copy in first:
        copy.start()
    for copy in first:
        copy.wait()
    for copy in second:
        copy.start()
    second[0].wait()

    small = TILE

    def forward(block, carry):
        rows = pl.ds(pl.multiple_of(block * small, small), small)
        wide = xh[rows, :].astype(F32)
        normed = (wide * scale_of(wide)).astype(BF16)
        a[0, rows, :] = normed
        for j in range(s.units):
            cols = pl.ds(j * TILE, TILE)
            gs[j % 2] = dot(normed, dg[pl.ds(0, s.d), cols])
            us[j % 2] = dot(normed, dg[pl.ds(s.d, s.d), cols])
            for r in range(0, small, 32):
                g = gs[j % 2, pl.ds(r, 32), :]
                hs[pl.ds(r, 32), cols] = (g * jax.nn.sigmoid(g) * us[j % 2, pl.ds(r, 32), :]).astype(BF16)
        ps[0] = dot(hs[...], du[:, pl.ds(0, s.d)])
        for r in range(0, small, 32):
            part = pl.ds(block * small + r, 32)
            h = (xh[part, :].astype(F32) + ps[0, pl.ds(r, 32), :].astype(BF16).astype(F32)).astype(BF16)
            xh[part, :] = h
            wide = h.astype(F32)
            a[1, part, :] = (wide * scale_of(wide)).astype(BF16)
        a_t[:, rows] = a[1, rows, :].T
        dh_t[:, rows] = dh[rows, :].T
        return carry

    lax.fori_loop(0, s.tokens // small, forward, 0)
    for copy in second[1:]:
        copy.wait()
    pl.semaphore_wait(barrier, 2)

    quarter = s.tokens // 4

    def inner(layer, unit, block):
        cols = pl.ds(pl.multiple_of(unit * TILE, TILE), TILE)
        for half in range(quarter // TILE):
            at = block * quarter + half * TILE
            rows = pl.ds(at, TILE)
            gs[half] = dot(a[layer, rows, :], wg[:, cols])
            us[half] = dot(a[layer, rows, :], wu[:, cols])
            ds[half] = dot_t(dh[rows, :], wd[cols, :]).astype(BF16)
            for r in range(0, TILE, 32):
                part = pl.ds(r, 32)
                g, u, by = gs[half, part, :], us[half, part, :], ds[half, part, :].astype(F32)
                sig = jax.nn.sigmoid(g)
                silu = g * sig
                rows = pl.ds(at + r, 32)
                hid[rows, :] = (silu * u).astype(BF16)
                du[rows, cols] = (by * silu).astype(BF16)
                dg[rows, cols] = (by * u * (sig + silu * (1.0 - sig))).astype(BF16)

    def keep_across(slot, which, value):
        for chunk in range(s.n):
            for half in range(s.halves):
                own[slot, which, chunk, pl.ds(half * s.rows, s.rows), :] = value[
                    chunk * s.rows : (chunk + 1) * s.rows, half * LANES : (half + 1) * LANES
                ]

    def by_gate(unit, slot):
        cols = pl.ds(pl.multiple_of(unit * TILE, TILE), TILE)
        keep_across(slot, 0, dot(a_t[...], dg[:, cols]).astype(BF16))

    def by_up(unit, slot):
        cols = pl.ds(pl.multiple_of(unit * TILE, TILE), TILE)
        keep_across(slot, 1, dot(a_t[...], du[:, cols]).astype(BF16))

    def by_down(slot):
        value = dot(dh_t[...], hid[...]).T.astype(BF16)
        for which in range(2):
            for chunk in range(s.n):
                top = (which * s.n + chunk) * s.down
                for fifth in range(s.fifths):
                    own[slot, which, chunk, pl.ds(s.halves * s.rows + fifth * s.down, s.down), :] = value[
                        top : top + s.down, fifth * LANES : (fifth + 1) * LANES
                    ]

    def back_through_norm(block):
        at = block * TILE
        rows = pl.ds(pl.multiple_of(at, TILE), TILE)
        ps[0] = dot_t(dg[rows, :], wg[...])
        ps[1] = dot_t(du[rows, :], wu[...])
        for r in range(0, TILE, 32):
            part, here = pl.ds(r, 32), pl.ds(at + r, 32)
            by_a = (ps[0, part, :].astype(BF16).astype(F32) + ps[1, part, :].astype(BF16).astype(F32)).astype(BF16).astype(F32)
            wide = xh[here, :].astype(F32)
            scale = scale_of(wide)
            by = scale * by_a - wide * (scale * scale * scale * jnp.mean(wide * by_a, -1, keepdims=True))
            dh[here, :] = (dh[here, :].astype(F32) + by.astype(BF16).astype(F32)).astype(BF16)
        dh_t[:, rows] = dh[rows, :].T
        a_t[:, rows] = a[0, rows, :].T

    late = s.units + GAP

    def is_unit(u):
        return ((u >= 0) & (u < s.units)) | ((u >= late) & (u < late + s.units))

    def chunk_of(way, hop):
        return lax.rem(me + (s.n - 1 - hop if way == 0 else 1 + hop), s.n)

    def send(u, hop, way):
        slot = lax.rem(u, SLOTS)
        return pltpu.make_async_remote_copy(
            src_ref=own.at[slot, way, chunk_of(way, hop)],
            dst_ref=got.at[slot, hop, way],
            send_sem=send_sem.at[slot, way],
            recv_sem=recv_sem.at[slot, hop, way],
            device_id={"dp": towards[way]},
            device_id_type=pl.DeviceIdType.MESH,
        )

    def hop(u, number):
        @pl.when(is_unit(u))
        def _():
            slot = lax.rem(u, SLOTS)
            for way in range(2):
                if number > 0:
                    before = send(u, number - 1, way)
                    before.wait_recv()
                    mine = own[slot, way, chunk_of(way, number)].astype(F32)
                    total = (mine + got[slot, number - 1, way].astype(F32)).astype(BF16)
                    if number < s.n - 1:
                        own[slot, way, chunk_of(way, number)] = total
                    else:
                        final[lax.select(u < late, 1, 0), lax.select(u < late, u, u - late), way] = total
                    before.wait_send()
            if number < s.n - 1:
                for way in range(2):
                    send(u, number, way).start()

    def period(q, carry):
        early = q < s.units
        real = is_unit(q)
        layer = lax.select(early, 1, 0)
        unit = lax.select(early, q, q - late)
        slot = lax.rem(q, SLOTS)
        between = (q >= s.units) & (q < late)
        plan = ([(2, 2)], [(3, 4)], [(4, 6)], [(1, 1)], [(2, 3)], [(3, 5)], [(4, 7), (0, 0)])
        for k in range(7):
            @pl.when(real)
            def _():
                if k == 0:
                    @pl.when(q >= late)
                    def _():
                        for copy in pieces(unit):
                            copy.wait()
                if k < 4:
                    inner(layer, unit, k)
                elif k == 4:
                    by_gate(unit, slot)
                elif k == 5:
                    by_up(unit, slot)
                else:
                    by_down(slot)

            if k < 4:
                @pl.when(between)
                def _():
                    back_through_norm((q - s.units) * 4 + k)

            if k == 3:
                @pl.when(q == late - 1)
                def _():
                    def fetch(piece, carry):
                        for copy in pieces(piece):
                            copy.start()
                        return carry
                    lax.fori_loop(0, s.units, fetch, 0)

            for back, number in plan[k]:
                hop(q - back, number)
        return carry

    def pieces(unit):
        cols = pl.ds(pl.multiple_of(unit * TILE, TILE), TILE)
        return [
            pltpu.make_async_copy(wg_hbm.at[0, :, cols], wg.at[:, cols], w_sem.at[0, unit]),
            pltpu.make_async_copy(wu_hbm.at[0, :, cols], wu.at[:, cols], w_sem.at[1, unit]),
            pltpu.make_async_copy(wd_hbm.at[0, cols, :], wd.at[cols, :], w_sem.at[2, unit]),
        ]

    lax.fori_loop(0, late + s.units + 4, period, 0)

    half = s.units // 2
    outs = [
        pltpu.make_async_copy(final.at[:, pl.ds(part * half, half), way], (own_x, own_y)[part][way], out_sem.at[part, way])
        for part in range(2)
        for way in range(2)
    ]
    for copy in outs:
        copy.start()
    for copy in outs:
        copy.wait()


def reduced_shards(s, x, dy, w_gate, w_up, w_down):
    shard = jax.ShapeDtypeStruct((s.layers, s.units // 2, s.message, LANES), BF16)
    d, t, ff = s.d, s.tokens, s.ff
    any_space = pl.BlockSpec(memory_space=pl.ANY)
    out = pl.pallas_call(
        functools.partial(step_kernel, s),
        out_shape=(shard,) * 4,
        in_specs=[any_space] * 5,
        out_specs=(any_space,) * 4,
        scratch_shapes=[
            pltpu.VMEM((d, ff), BF16),
            pltpu.VMEM((d, ff), BF16),
            pltpu.VMEM((ff, d), BF16),
            pltpu.VMEM((t, d), BF16),
            pltpu.VMEM((2, t, d), BF16),
            pltpu.VMEM((d, t), BF16),
            pltpu.VMEM((t, d), BF16),
            pltpu.VMEM((d, t), BF16),
            pltpu.VMEM((t, ff), BF16),
            pltpu.VMEM((t, ff), BF16),
            pltpu.VMEM((t, TILE), BF16),
            pltpu.VMEM((SLOTS, 2, s.n, s.message, LANES), BF16),
            pltpu.VMEM((SLOTS, s.n - 1, 2, s.message, LANES), BF16),
            pltpu.VMEM((s.layers, s.units, 2, s.message, LANES), BF16),
            pltpu.VMEM((2, TILE, TILE), F32),
            pltpu.VMEM((2, TILE, TILE), F32),
            pltpu.VMEM((2, TILE, TILE), BF16),
            pltpu.VMEM((TILE, ff), BF16),
            pltpu.VMEM((2, TILE, d), F32),
            pltpu.SemaphoreType.DMA((8,)),
            pltpu.SemaphoreType.DMA((3, s.units)),
            pltpu.SemaphoreType.DMA((SLOTS, 2)),
            pltpu.SemaphoreType.DMA((SLOTS, s.n - 1, 2)),
            pltpu.SemaphoreType.DMA((2, 2)),
        ],
        compiler_params=pltpu.CompilerParams(collective_id=0, has_side_effects=True, vmem_limit_bytes=67043328),
    )(x, dy, w_gate, w_up, w_down)
    return [out[0:2], out[2:4]]


def adamw(w, m, v, g):
    m = 0.9 * m + 0.1 * g
    v = 0.95 * v + 0.05 * g * g
    step = m * lax.rsqrt(v + 1e-8) + 0.1 * w
    return (w - 0.02 * step).astype(BF16), m, v


def adamw_kernel(s, where_ref, from_left, from_right, *refs):
    across, down = (refs[0:3], refs[3:6]), refs[6:9]
    outs = refs[len(refs) - 9 :]
    across_out, down_out = (outs[0:3], outs[3:6]), outs[6:9]

    for way, message in enumerate((from_left, from_right)):
        @pl.when(pl.program_id(0) == way)
        def _():
            def unit_step(unit, carry):
                for half in range(s.halves):
                    g = message[0, unit, pl.ds(half * s.rows, s.rows), :].astype(F32)
                    cols = pl.ds(pl.multiple_of(unit * TILE + half * LANES, LANES), LANES)
                    w, m, v = (ref[0, :, cols] for ref in across[way])
                    new = adamw(w.astype(F32), m, v, g)
                    for ref, value in zip(across_out[way], new, strict=True):
                        ref[0, :, cols] = value
                for fifth in range(s.fifths):
                    g = message[0, unit, pl.ds(s.halves * s.rows + fifth * s.down, s.down), :].astype(F32)
                    cols = pl.ds(fifth * LANES, LANES)
                    w, m, v = (ref[0, unit, 0, 0, :, cols] for ref in down)
                    new = adamw(w.astype(F32), m, v, g)
                    for ref, value in zip(down_out, new, strict=True):
                        ref[0, unit, 0, 0, :, cols] = value
                return carry

            lax.fori_loop(0, s.units // 2, unit_step, 0)


def adamw_on(s, part, hop, messages, state, so_far):
    me = lax.axis_index("dp")
    where = jnp.stack([lax.rem(me + s.n - hop, s.n), lax.rem(me + hop, s.n)]).astype(jnp.int32)
    half = s.units // 2
    last = s.layers - 1
    spec_across = (
        pl.BlockSpec((1, s.rows, half * TILE), lambda way, layer, at: (jnp.where(way == 0, layer, last), at[0], part)),
        pl.BlockSpec((1, s.rows, half * TILE), lambda way, layer, at: (jnp.where(way == 0, 0, layer), at[1], part)),
    )
    spec_down = pl.BlockSpec((1, half, 1, 1, s.down, s.d), lambda way, layer, at: (layer, part, way, at[way], 0, 0))
    spec_message = (
        pl.BlockSpec((1, half, s.message, LANES), lambda way, layer, at: (jnp.where(way == 0, layer, last), 0, 0, 0)),
        pl.BlockSpec((1, half, s.message, LANES), lambda way, layer, at: (jnp.where(way == 0, 0, layer), 0, 0, 0)),
    )
    specs = [spec_across[0]] * 3 + [spec_across[1]] * 3 + [spec_down] * 3
    flat = [one for group in state for one in group]
    shapes = [jax.ShapeDtypeStruct(one.shape, one.dtype) for one in flat]
    in_specs = list(spec_message) + specs
    args = [*messages, *flat]
    aliases = {}
    if so_far is not None:
        aliases = {1 + len(args) + i: i for i in range(9)}
        args += so_far
        in_specs += [pl.BlockSpec(memory_space=pl.ANY)] * 9
    numbers = 2 * s.layers * half * s.message * LANES
    return list(
        pl.pallas_call(
            functools.partial(adamw_kernel, s),
            out_shape=shapes,
            grid_spec=pltpu.PrefetchScalarGridSpec(num_scalar_prefetch=1, grid=(2, s.layers), in_specs=in_specs, out_specs=specs),
            input_output_aliases=aliases,
            cost_estimate=pl.CostEstimate(flops=numbers * 20 * 1000, bytes_accessed=numbers * 22, transcendentals=numbers),
        )(where, *args)
    )


def solution(mesh):
    n = mesh.shape["dp"]

    def step(x, dy, *arrays):
        weights, m, v = (arrays[i : i + 3] for i in (0, 3, 6))
        s = Sizes(mesh, x, weights[0])
        halves = reduced_shards(s, x, dy, *weights)
        by_chunk = (s.layers, s.units, 2, s.n, s.down, s.d)
        state = [list(group) for group in zip(weights, m, v, strict=True)]
        state[2] = [one.reshape(by_chunk) for one in state[2]]
        rings = ([(i, (i + 1) % n) for i in range(n)], [(i, (i - 1) % n) for i in range(n)])
        out = None
        for hop in range(n):
            now = halves
            if hop < n - 1:
                halves = [[lax.ppermute(one, "dp", ring) for one, ring in zip(pair, rings, strict=True)] for pair in halves]
            for part in range(2):
                out = adamw_on(s, part, hop, now[part], state, out)
        out[6:9] = [one.reshape(weights[2].shape) for one in out[6:9]]
        return tuple(out[3 * which + i] for i in range(3) for which in range(3))

    return jax.shard_map(
        step,
        mesh=mesh,
        in_specs=(P(("rep", "dp"), None, None),) * 2 + (P(None, None, None),) * 9,
        out_specs=(P("rep", None, None),) * 9,
        check_vma=False,
    )
```

time: 616 us -> 392 us (0.64); the launches traced: 606 us -> 390 us
  Pallas kernels: 0 us -> 336 us
  waiting for transfers between devices: 324 us -> 0.52 us
  matrix products: 199 us -> 0 us
  other arithmetic: 59.8 us -> 4.81 us
  starting transfers between devices: 0.06 us -> 46.1 us
  between operations: 14.8 us -> 1.31 us
  local copies, waits for them, and re-layouts: 9.26 us -> 2.04 us
    pallas_call x0 -> x17, Pallas kernels: none -> 336 us  [the longest x1 222 us: reduced_shards(): pl.pallas_call(functools.partial(step_kernel, s), out_shape=(shard,) * 4,...]
    psum x1 -> x0, waiting for transfers between devices: 324 us -> none  [step(): summed[number] = [lax.psum(by_w[name], 'dp') for name in NAMES]]
    dot_general x15 -> x0, matrix products: 199 us -> none  [the longest x5 75.1 us: layer(): gate = jnp.dot(a, w['w_gate'], preferred_element_type=jnp.float32)]
    convert_element_type x2 -> x0, other arithmetic: 57.1 us -> none  [adamw(): return ((w - 0.02 * step).astype(jnp.bfloat16), m, v)]
    ppermute x0 -> x28, starting transfers between devices: none -> 46.1 us  [step(): lax.ppermute(one, 'dp', ring)]
    unnamed x40 -> x46, local copies, waits for them, and re-layouts: 9.26 us -> 2.04 us
  transfers between devices with their start and end apart: 1 -> 28, of which waited for: 1 -> 1; matrix products, arithmetic and copies ran while one was open for 0% -> 1% of each run, Pallas kernels for 0% -> 27%
where the time goes in v1:
time: 392 us; the launch traced here: 390 us
  Pallas kernels  336 us (86%)
  starting transfers between devices  46.1 us (12%)
  other arithmetic  4.81 us (1%)
    pallas_call x1, Pallas kernels, reduced_shards(): pl.pallas_call(functools.partial(step_kernel, s), out_shape=(shard,) * 4,...  222 us
    pallas_call x16, Pallas kernels, adamw_on(): pl.pallas_call(functools.partial(adamw_kernel, s), out_shape=shapes, grid...  113 us
    ppermute x28, starting transfers between devices, step(): lax.ppermute(one, 'dp', ring)  46.1 us
  transfers between devices with their start and end apart: 28, of which 1 were waited for; matrix products, arithmetic and copies ran while one was open for 1% of the time, Pallas kernels for 27%

profile of v1, /device:TPU:22, one launch (start us, length us, event | category | flops | bytes accessed | tf_op | source)
XLA Modules:
  0.0 390.4 jit_solution(10717735204579071384)
XLA Ops:
  0.6 222.2 %shard_map.178 = (bf16[2,4,240,128]{3,2,1,0:T(8,128)(2,1)}, bf16[2,4,240,128]{3,2,1,0:T(8,128)(2,1)}, bf16[2,4,240,128]{3,2,1,0:T(8,128)(2,1)}, bf16[2,4,240,128]{3,2,1,0:T(8,128)(2,1)}) custom-call(bf16[1,2048,640]{2,1,0:T(8,128)(2,1)} %x_hbm.1, bf16[1,2048,640]{2,1,0:T(8,128)(2,1)} %dy_hbm.1, bf16[2,640,2048]{2,1,0:T(8,128)(2,1)} %refs_0_.31, ...), custom_call_target="tpu_custom_call" | custom-call | tf_op jit(solution)/shard_map/pallas_call | solution.py:270
  226.2 3.2 collective-permute-start.7
  231.1 7.0 %shard_map.179 = (bf16[2,640,2048]{2,1,0:T(8,128)(2,1)}, f32[2,640,2048]{2,1,0:T(8,128)}, f32[2,640,2048]{2,1,0:T(8,128)}, bf16[2,640,2048]{2,1,0:T(8,128)(2,1)}...) custom-call(s32[2]{0:T(128)} %pad_add_fusion.7.where_ref, ...), custom_call_target="tpu_custom_call" | custom-call | flops 9830400000 | bytes 10813440 | tf_op jit(solution)/shard_map/pallas_call | solution.py:367
  238.2 7.1 %shard_map.180 = (bf16[2,640,2048]{2,1,0:T(8,128)(2,1)}, f32[2,640,2048]{2,1,0:T(8,128)}, f32[2,640,2048]{2,1,0:T(8,128)}, bf16[2,640,2048]{2,1,0:T(8,128)(2,1)}...) custom-call(s32[2]{0:T(128)} %pad_add_fusion.7.where_ref, ...), custom_call_target="tpu_custom_call", output_to_operand_aliasing={{0}: (12, {}), {1}: (13, {}), {2}: (14, {}), {3}: (15, {}),... | custom-call | flops 9830400000 | bytes 10813440 | tf_op jit(solution)/shard_map/pallas_call | solution.py:367
  254.9 7.1 %shard_map.181 = (bf16[2,640,2048]{2,1,0:T(8,128)(2,1)}, f32[2,640,2048]{2,1,0:T(8,128)}, f32[2,640,2048]{2,1,0:T(8,128)}, bf16[2,640,2048]{2,1,0:T(8,128)(2,1)}...) custom-call(s32[2]{0:T(128)} %pad_add_fusion.6.where_ref, ...), custom_call_target="tpu_custom_call", output_to_operand_aliasing={{0}: (12, {}), {1}: (13, {}), {2}: (14, {}), {3}: (15, {}),... | custom-call | flops 9830400000 | bytes 10813440 | tf_op jit(solution)/shard_map/pallas_call | solution.py:367
  262.0 7.1 %shard_map.182 = (bf16[2,640,2048]{2,1,0:T(8,128)(2,1)}, f32[2,640,2048]{2,1,0:T(8,128)}, f32[2,640,2048]{2,1,0:T(8,128)}, bf16[2,640,2048]{2,1,0:T(8,128)(2,1)}...) custom-call(s32[2]{0:T(128)} %pad_add_fusion.6.where_ref, ...), custom_call_target="tpu_custom_call", output_to_operand_aliasing={{0}: (12, {}), {1}: (13, {}), {2}: (14, {}), {3}: (15, {}),... | custom-call | flops 9830400000 | bytes 10813440 | tf_op jit(solution)/shard_map/pallas_call | solution.py:367
  272.5 3.2 collective-permute-start.9
  275.7 7.0 %shard_map.183 = (bf16[2,640,2048]{2,1,0:T(8,128)(2,1)}, f32[2,640,2048]{2,1,0:T(8,128)}, f32[2,640,2048]{2,1,0:T(8,128)}, bf16[2,640,2048]{2,1,0:T(8,128)(2,1)}...) custom-call(s32[2]{0:T(128)} %pad_add_fusion.5.where_ref, ...), custom_call_target="tpu_custom_call", output_to_operand_aliasing={{0}: (12, {}), {1}: (13, {}), {2}: (14, {}), {3}: (15, {}),... | custom-call | flops 9830400000 | bytes 10813440 | tf_op jit(solution)/shard_map/pallas_call | solution.py:367
  282.8 7.1 %shard_map.184 = (bf16[2,640,2048]{2,1,0:T(8,128)(2,1)}, f32[2,640,2048]{2,1,0:T(8,128)}, f32[2,640,2048]{2,1,0:T(8,128)}, bf16[2,640,2048]{2,1,0:T(8,128)(2,1)}...) custom-call(s32[2]{0:T(128)} %pad_add_fusion.5.where_ref, ...), custom_call_target="tpu_custom_call", output_to_operand_aliasing={{0}: (12, {}), {1}: (13, {}), {2}: (14, {}), {3}: (15, {}),... | custom-call | flops 9830400000 | bytes 10813440 | tf_op jit(solution)/shard_map/pallas_call | solution.py:367
  295.3 7.0 %shard_map.185 = (bf16[2,640,2048]{2,1,0:T(8,128)(2,1)}, f32[2,640,2048]{2,1,0:T(8,128)}, f32[2,640,2048]{2,1,0:T(8,128)}, bf16[2,640,2048]{2,1,0:T(8,128)(2,1)}...) custom-call(s32[2]{0:T(128)} %pad_add_fusion.4.where_ref, ...), custom_call_target="tpu_custom_call", output_to_operand_aliasing={{0}: (12, {}), {1}: (13, {}), {2}: (14, {}), {3}: (15, {}),... | custom-call | flops 9830400000 | bytes 10813440 | tf_op jit(solution)/shard_map/pallas_call | solution.py:367
  302.3 7.1 %shard_map.186 = (bf16[2,640,2048]{2,1,0:T(8,128)(2,1)}, f32[2,640,2048]{2,1,0:T(8,128)}, f32[2,640,2048]{2,1,0:T(8,128)}, bf16[2,640,2048]{2,1,0:T(8,128)(2,1)}...) custom-call(s32[2]{0:T(128)} %pad_add_fusion.4.where_ref, ...), custom_call_target="tpu_custom_call", output_to_operand_aliasing={{0}: (12, {}), {1}: (13, {}), {2}: (14, {}), {3}: (15, {}),... | custom-call | flops 9830400000 | bytes 10813440 | tf_op jit(solution)/shard_map/pallas_call | solution.py:367
  313.3 3.7 collective-permute-start.11
  317.0 7.1 %shard_map.187 = (bf16[2,640,2048]{2,1,0:T(8,128)(2,1)}, f32[2,640,2048]{2,1,0:T(8,128)}, f32[2,640,2048]{2,1,0:T(8,128)}, bf16[2,640,2048]{2,1,0:T(8,128)(2,1)}...) custom-call(s32[2]{0:T(128)} %pad_add_fusion.3.where_ref, ...), custom_call_target="tpu_custom_call", output_to_operand_aliasing={{0}: (12, {}), {1}: (13, {}), {2}: (14, {}), {3}: (15, {}),... | custom-call | flops 9830400000 | bytes 10813440 | tf_op jit(solution)/shard_map/pallas_call | solution.py:367
  324.1 7.1 %shard_map.188 = (bf16[2,640,2048]{2,1,0:T(8,128)(2,1)}, f32[2,640,2048]{2,1,0:T(8,128)}, f32[2,640,2048]{2,1,0:T(8,128)}, bf16[2,640,2048]{2,1,0:T(8,128)(2,1)}...) custom-call(s32[2]{0:T(128)} %pad_add_fusion.3.where_ref, ...), custom_call_target="tpu_custom_call", output_to_operand_aliasing={{0}: (12, {}), {1}: (13, {}), {2}: (14, {}), {3}: (15, {}),... | custom-call | flops 9830400000 | bytes 10813440 | tf_op jit(solution)/shard_map/pallas_call | solution.py:367
  331.7 3.3 collective-permute-start.26
  335.0 3.7 collective-permute-start.12
  338.7 7.1 %shard_map.189 = (bf16[2,640,2048]{2,1,0:T(8,128)(2,1)}, f32[2,640,2048]{2,1,0:T(8,128)}, f32[2,640,2048]{2,1,0:T(8,128)}, bf16[2,640,2048]{2,1,0:T(8,128)(2,1)}...) custom-call(s32[2]{0:T(128)} %pad_add_fusion.2.where_ref, ...), custom_call_target="tpu_custom_call", output_to_operand_aliasing={{0}: (12, {}), {1}: (13, {}), {2}: (14, {}), {3}: (15, {}),... | custom-call | flops 9830400000 | bytes 10813440 | tf_op jit(solution)/shard_map/pallas_call | solution.py:367
  345.8 7.1 %shard_map.190 = (bf16[2,640,2048]{2,1,0:T(8,128)(2,1)}, f32[2,640,2048]{2,1,0:T(8,128)}, f32[2,640,2048]{2,1,0:T(8,128)}, bf16[2,640,2048]{2,1,0:T(8,128)(2,1)}...) custom-call(s32[2]{0:T(128)} %pad_add_fusion.2.where_ref, ...), custom_call_target="tpu_custom_call", output_to_operand_aliasing={{0}: (12, {}), {1}: (13, {}), {2}: (14, {}), {3}: (15, {}),... | custom-call | flops 9830400000 | bytes 10813440 | tf_op jit(solution)/shard_map/pallas_call | solution.py:367
  353.1 3.3 collective-permute-start.27
  356.3 3.4 collective-permute-start.13
  359.8 7.1 %shard_map.191 = (bf16[2,640,2048]{2,1,0:T(8,128)(2,1)}, f32[2,640,2048]{2,1,0:T(8,128)}, f32[2,640,2048]{2,1,0:T(8,128)}, bf16[2,640,2048]{2,1,0:T(8,128)(2,1)}...) custom-call(s32[2]{0:T(128)} %pad_add_fusion.1.where_ref, ...), custom_call_target="tpu_custom_call", output_to_operand_aliasing={{0}: (12, {}), {1}: (13, {}), {2}: (14, {}), {3}: (15, {}),... | custom-call | flops 9830400000 | bytes 10813440 | tf_op jit(solution)/shard_map/pallas_call | solution.py:367
  366.9 7.1 %shard_map.192 = (bf16[2,640,2048]{2,1,0:T(8,128)(2,1)}, f32[2,640,2048]{2,1,0:T(8,128)}, f32[2,640,2048]{2,1,0:T(8,128)}, bf16[2,640,2048]{2,1,0:T(8,128)(2,1)}...) custom-call(s32[2]{0:T(128)} %pad_add_fusion.1.where_ref, ...), custom_call_target="tpu_custom_call", output_to_operand_aliasing={{0}: (12, {}), {1}: (13, {}), {2}: (14, {}), {3}: (15, {}),... | custom-call | flops 9830400000 | bytes 10813440 | tf_op jit(solution)/shard_map/pallas_call | solution.py:367
  375.1 7.0 %shard_map.193 = (bf16[2,640,2048]{2,1,0:T(8,128)(2,1)}, f32[2,640,2048]{2,1,0:T(8,128)}, f32[2,640,2048]{2,1,0:T(8,128)}, bf16[2,640,2048]{2,1,0:T(8,128)(2,1)}...) custom-call(s32[2]{0:T(128)} %pad_add_fusion.where_ref, ...), custom_call_target="tpu_custom_call", output_to_operand_aliasing={{0}: (12, {}), {1}: (13, {}), {2}: (14, {}), {3}: (15, {}),... | custom-call | flops 9830400000 | bytes 10813440 | tf_op jit(solution)/shard_map/pallas_call | solution.py:367
  383.1 7.1 %shard_map.194 = (bf16[2,640,2048]{2,1,0:T(8,128)(2,1)}, f32[2,640,2048]{2,1,0:T(8,128)}, f32[2,640,2048]{2,1,0:T(8,128)}, bf16[2,640,2048]{2,1,0:T(8,128)(2,1)}...) custom-call(s32[2]{0:T(128)} %pad_add_fusion.where_ref, ...), custom_call_target="tpu_custom_call", output_to_operand_aliasing={{0}: (12, {}), {1}: (13, {}), {2}: (14, {}), {3}: (15, {}),... | custom-call | flops 9830400000 | bytes 10813440 | tf_op jit(solution)/shard_map/pallas_call | solution.py:367
  (103 shorter events, 29.6 us)
Async XLA Ops:
  222.8 25.6 %collective-permute-start.14 = (bf16[2,4,240,128]{3,2,1,0:T(8,128)(2,1)}, bf16[2,4,240,128]{3,2,1,0:T(8,128)(2,1)S(1)}, u32[]{:S(2)}, u32[]{:S(2)}) collective-permute-start(bf16[2,4,240,128]{3,2,1,0:T(8,128)(2,1)} %get-tuple-element.159.from_left), channel_id=1, source_target_pairs={{0,1},{1,2},{2,3},{3,4},{4,5},{5,6},{6,7},{7,0},{8,9},{9,10},{10,1... | collective-permute-start | bytes 1474568 | tf_op jit(solution)/shard_map/ppermute | solution.py:392
  223.5 24.9 %collective-permute-start.21 = (bf16[2,4,240,128]{3,2,1,0:T(8,128)(2,1)}, bf16[2,4,240,128]{3,2,1,0:T(8,128)(2,1)S(1)}, u32[]{:S(2)}, u32[]{:S(2)}) collective-permute-start(bf16[2,4,240,128]{3,2,1,0:T(8,128)(2,1)} %get-tuple-element.160.from_right), channel_id=1, source_target_pairs={{0,7},{1,0},{2,1},{3,2},{4,3},{5,4},{6,5},{7,6},{8,15},{9,8},{10,9... | collective-permute-start | bytes 1474568 | tf_op jit(solution)/shard_map/ppermute | solution.py:392
  226.1 25.5 %collective-permute-start = (bf16[2,4,240,128]{3,2,1,0:T(8,128)(2,1)}, bf16[2,4,240,128]{3,2,1,0:T(8,128)(2,1)S(1)}, u32[]{:S(2)}, u32[]{:S(2)}) collective-permute-start(bf16[2,4,240,128]{3,2,1,0:T(8,128)(2,1)} %get-tuple-element.157.from_left), channel_id=1, source_target_pairs={{0,1},{1,2},{2,3},{3,4},{4,5},{5,6},{6,7},{7,0},{8,9},{9,10},{10,1... | collective-permute-start | bytes 1474568 | tf_op jit(solution)/shard_map/ppermute | solution.py:392
  226.2 25.5 %collective-permute-start.7 = (bf16[2,4,240,128]{3,2,1,0:T(8,128)(2,1)}, bf16[2,4,240,128]{3,2,1,0:T(8,128)(2,1)S(1)}, u32[]{:S(2)}, u32[]{:S(2)}) collective-permute-start(bf16[2,4,240,128]{3,2,1,0:T(8,128)(2,1)} %get-tuple-element.158.from_right), channel_id=1, source_target_pairs={{0,7},{1,0},{2,1},{3,2},{4,3},{5,4},{6,5},{7,6},{8,15},{9,8},{10,9... | collective-permute-start | bytes 1474568 | tf_op jit(solution)/shard_map/ppermute | solution.py:392
  248.4 20.8 %collective-permute-start.22 = (bf16[2,4,240,128]{3,2,1,0:T(8,128)(2,1)S(1)}, bf16[2,4,240,128]{3,2,1,0:T(8,128)(2,1)S(1)}, u32[]{:S(2)}, u32[]{:S(2)}) collective-permute-start(bf16[2,4,240,128]{3,2,1,0:T(8,128)(2,1)S(1)} %collective-permute-done.21.from_right), channel_id=1, source_target_pairs={{0,7},{1,0},{2,1},{3,2},{4,3},{5,4},{6,5},{7,6},{8,15},{9,8},{10,9... | collective-permute-start | bytes 1474568 | tf_op jit(solution)/shard_map/ppermute | solution.py:392
  251.6 20.8 %collective-permute-start.1 = (bf16[2,4,240,128]{3,2,1,0:T(8,128)(2,1)S(1)}, bf16[2,4,240,128]{3,2,1,0:T(8,128)(2,1)S(1)}, u32[]{:S(2)}, u32[]{:S(2)}) collective-permute-start(bf16[2,4,240,128]{3,2,1,0:T(8,128)(2,1)S(1)} %collective-permute-done.from_left), channel_id=1, source_target_pairs={{0,1},{1,2},{2,3},{3,4},{4,5},{5,6},{6,7},{7,0},{8,9},{9,10},{10,1... | collective-permute-start | bytes 1474568 | tf_op jit(solution)/shard_map/ppermute | solution.py:392
  251.7 20.8 %collective-permute-start.8 = (bf16[2,4,240,128]{3,2,1,0:T(8,128)(2,1)S(1)}, bf16[2,4,240,128]{3,2,1,0:T(8,128)(2,1)}, u32[]{:S(2)}, u32[]{:S(2)}) collective-permute-start(bf16[2,4,240,128]{3,2,1,0:T(8,128)(2,1)S(1)} %collective-permute-done.7.from_right), channel_id=1, source_target_pairs={{0,7},{1,0},{2,1},{3,2},{4,3},{5,4},{6,5},{7,6},{8,15},{9,8},{10,9... | collective-permute-start | bytes 1474568 | tf_op jit(solution)/shard_map/ppermute | solution.py:392
  269.1 20.8 %collective-permute-start.16 = (bf16[2,4,240,128]{3,2,1,0:T(8,128)(2,1)S(1)}, bf16[2,4,240,128]{3,2,1,0:T(8,128)(2,1)S(1)}, u32[]{:S(2)}, u32[]{:S(2)}) collective-permute-start(bf16[2,4,240,128]{3,2,1,0:T(8,128)(2,1)S(1)} %collective-permute-done.15.from_left), channel_id=1, source_target_pairs={{0,1},{1,2},{2,3},{3,4},{4,5},{5,6},{6,7},{7,0},{8,9},{9,10},{10,1... | collective-permute-start | bytes 1474568 | tf_op jit(solution)/shard_map/ppermute | solution.py:392
  269.3 20.8 %collective-permute-start.23 = (bf16[2,4,240,128]{3,2,1,0:T(8,128)(2,1)S(1)}, bf16[2,4,240,128]{3,2,1,0:T(8,128)(2,1)S(1)}, u32[]{:S(2)}, u32[]{:S(2)}) collective-permute-start(bf16[2,4,240,128]{3,2,1,0:T(8,128)(2,1)S(1)} %collective-permute-done.22.from_right), channel_id=1, source_target_pairs={{0,7},{1,0},{2,1},{3,2},{4,3},{5,4},{6,5},{7,6},{8,15},{9,8},{10,9... | collective-permute-start | bytes 1474568 | tf_op jit(solution)/shard_map/ppermute | solution.py:392
  272.5 20.9 %collective-permute-start.2 = (bf16[2,4,240,128]{3,2,1,0:T(8,128)(2,1)S(1)}, bf16[2,4,240,128]{3,2,1,0:T(8,128)(2,1)S(1)}, u32[]{:S(2)}, u32[]{:S(2)}) collective-permute-start(bf16[2,4,240,128]{3,2,1,0:T(8,128)(2,1)S(1)} %collective-permute-done.1.from_left), channel_id=1, source_target_pairs={{0,1},{1,2},{2,3},{3,4},{4,5},{5,6},{6,7},{7,0},{8,9},{9,10},{10,1... | collective-permute-start | bytes 1474568 | tf_op jit(solution)/shard_map/ppermute | solution.py:392
  272.5 20.8 %collective-permute-start.9 = (bf16[2,4,240,128]{3,2,1,0:T(8,128)(2,1)}, bf16[2,4,240,128]{3,2,1,0:T(8,128)(2,1)}, u32[]{:S(2)}, u32[]{:S(2)}) collective-permute-start(bf16[2,4,240,128]{3,2,1,0:T(8,128)(2,1)} %collective-permute-done.8.from_right), channel_id=1, source_target_pairs={{0,7},{1,0},{2,1},{3,2},{4,3},{5,4},{6,5},{7,6},{8,15},{9,8},{10,9... | collective-permute-start | bytes 1474568 | tf_op jit(solution)/shard_map/ppermute | solution.py:392
  293.4 23.6 %collective-permute-start.3 = (bf16[2,4,240,128]{3,2,1,0:T(8,128)(2,1)S(1)}, bf16[2,4,240,128]{3,2,1,0:T(8,128)(2,1)S(1)}, u32[]{:S(2)}, u32[]{:S(2)}) collective-permute-start(bf16[2,4,240,128]{3,2,1,0:T(8,128)(2,1)S(1)} %collective-permute-done.2.from_left), channel_id=1, source_target_pairs={{0,1},{1,2},{2,3},{3,4},{4,5},{5,6},{6,7},{7,0},{8,9},{9,10},{10,1... | collective-permute-start | bytes 1474568 | tf_op jit(solution)/shard_map/ppermute | solution.py:392
  309.5 21.8 %collective-permute-start.18 = (bf16[2,4,240,128]{3,2,1,0:T(8,128)(2,1)S(1)}, bf16[2,4,240,128]{3,2,1,0:T(8,128)(2,1)S(1)}, u32[]{:S(2)}, u32[]{:S(2)}) collective-permute-start(bf16[2,4,240,128]{3,2,1,0:T(8,128)(2,1)S(1)} %collective-permute-done.17.from_left), channel_id=1, source_target_pairs={{0,1},{1,2},{2,3},{3,4},{4,5},{5,6},{6,7},{7,0},{8,9},{9,10},{10,1... | collective-permute-start | bytes 1474568 | tf_op jit(solution)/shard_map/ppermute | solution.py:392
  309.7 22.0 %collective-permute-start.25 = (bf16[2,4,240,128]{3,2,1,0:T(8,128)(2,1)S(1)}, bf16[2,4,240,128]{3,2,1,0:T(8,128)(2,1)S(1)}, u32[]{:S(2)}, u32[]{:S(2)}) collective-permute-start(bf16[2,4,240,128]{3,2,1,0:T(8,128)(2,1)S(1)} %collective-permute-done.24.from_right), channel_id=1, source_target_pairs={{0,7},{1,0},{2,1},{3,2},{4,3},{5,4},{6,5},{7,6},{8,15},{9,8},{10,9... | collective-permute-start | bytes 1474568 | tf_op jit(solution)/shard_map/ppermute | solution.py:392
  313.3 21.7 %collective-permute-start.11 = (bf16[2,4,240,128]{3,2,1,0:T(8,128)(2,1)S(1)}, bf16[2,4,240,128]{3,2,1,0:T(8,128)(2,1)}, u32[]{:S(2)}, u32[]{:S(2)}) collective-permute-start(bf16[2,4,240,128]{3,2,1,0:T(8,128)(2,1)S(1)} %collective-permute-done.10.from_right), channel_id=1, source_target_pairs={{0,7},{1,0},{2,1},{3,2},{4,3},{5,4},{6,5},{7,6},{8,15},{9,8},{10,9... | collective-permute-start | bytes 1474568 | tf_op jit(solution)/shard_map/ppermute | solution.py:392
  317.0 21.7 %collective-permute-start.4 = (bf16[2,4,240,128]{3,2,1,0:T(8,128)(2,1)S(1)}, bf16[2,4,240,128]{3,2,1,0:T(8,128)(2,1)}, u32[]{:S(2)}, u32[]{:S(2)}) collective-permute-start(bf16[2,4,240,128]{3,2,1,0:T(8,128)(2,1)S(1)} %collective-permute-done.3.from_left), channel_id=1, source_target_pairs={{0,1},{1,2},{2,3},{3,4},{4,5},{5,6},{6,7},{7,0},{8,9},{9,10},{10,1... | collective-permute-start | bytes 1474568 | tf_op jit(solution)/shard_map/ppermute | solution.py:392
  331.3 21.7 %collective-permute-start.19 = (bf16[2,4,240,128]{3,2,1,0:T(8,128)(2,1)S(1)}, bf16[2,4,240,128]{3,2,1,0:T(8,128)(2,1)}, u32[]{:S(2)}, u32[]{:S(2)}) collective-permute-start(bf16[2,4,240,128]{3,2,1,0:T(8,128)(2,1)S(1)} %collective-permute-done.18.from_left), channel_id=1, source_target_pairs={{0,1},{1,2},{2,3},{3,4},{4,5},{5,6},{6,7},{7,0},{8,9},{9,10},{10,1... | collective-permute-start | bytes 1474568 | tf_op jit(solution)/shard_map/ppermute | solution.py:392
  331.7 21.4 %collective-permute-start.26 = (bf16[2,4,240,128]{3,2,1,0:T(8,128)(2,1)S(1)}, bf16[2,4,240,128]{3,2,1,0:T(8,128)(2,1)S(1)}, u32[]{:S(2)}, u32[]{:S(2)}) collective-permute-start(bf16[2,4,240,128]{3,2,1,0:T(8,128)(2,1)S(1)} %collective-permute-done.25.from_right), channel_id=1, source_target_pairs={{0,7},{1,0},{2,1},{3,2},{4,3},{5,4},{6,5},{7,6},{8,15},{9,8},{10,9... | collective-permute-start | bytes 1474568 | tf_op jit(solution)/shard_map/ppermute | solution.py:392
  335.0 21.4 %collective-permute-start.12 = (bf16[2,4,240,128]{3,2,1,0:T(8,128)(2,1)}, bf16[2,4,240,128]{3,2,1,0:T(8,128)(2,1)S(1)}, u32[]{:S(2)}, u32[]{:S(2)}) collective-permute-start(bf16[2,4,240,128]{3,2,1,0:T(8,128)(2,1)} %collective-permute-done.11.from_right), channel_id=1, source_target_pairs={{0,7},{1,0},{2,1},{3,2},{4,3},{5,4},{6,5},{7,6},{8,15},{9,8},{10,9... | collective-permute-start | bytes 1474568 | tf_op jit(solution)/shard_map/ppermute | solution.py:392
  338.7 21.1 %collective-permute-start.5 = (bf16[2,4,240,128]{3,2,1,0:T(8,128)(2,1)}, bf16[2,4,240,128]{3,2,1,0:T(8,128)(2,1)S(1)}, u32[]{:S(2)}, u32[]{:S(2)}) collective-permute-start(bf16[2,4,240,128]{3,2,1,0:T(8,128)(2,1)} %collective-permute-done.4.from_left), channel_id=1, source_target_pairs={{0,1},{1,2},{2,3},{3,4},{4,5},{5,6},{6,7},{7,0},{8,9},{9,10},{10,1... | collective-permute-start | bytes 1474568 | tf_op jit(solution)/shard_map/ppermute | solution.py:392
  352.9 21.1 %collective-permute-start.20 = (bf16[2,4,240,128]{3,2,1,0:T(8,128)(2,1)}, bf16[2,4,240,128]{3,2,1,0:T(8,128)(2,1)S(1)}, u32[]{:S(2)}, u32[]{:S(2)}) collective-permute-start(bf16[2,4,240,128]{3,2,1,0:T(8,128)(2,1)} %collective-permute-done.19.from_left), channel_id=1, source_target_pairs={{0,1},{1,2},{2,3},{3,4},{4,5},{5,6},{6,7},{7,0},{8,9},{9,10},{10,1... | collective-permute-start | bytes 1474568 | tf_op jit(solution)/shard_map/ppermute | solution.py:392
  353.1 21.0 %collective-permute-start.27 = (bf16[2,4,240,128]{3,2,1,0:T(8,128)(2,1)S(1)}, bf16[2,4,240,128]{3,2,1,0:T(8,128)(2,1)S(1)}, u32[]{:S(2)}, u32[]{:S(2)}) collective-permute-start(bf16[2,4,240,128]{3,2,1,0:T(8,128)(2,1)S(1)} %collective-permute-done.26.from_right), channel_id=1, source_target_pairs={{0,7},{1,0},{2,1},{3,2},{4,3},{5,4},{6,5},{7,6},{8,15},{9,8},{10,9... | collective-permute-start | bytes 1474568 | tf_op jit(solution)/shard_map/ppermute | solution.py:392
  356.3 25.8 %collective-permute-start.13 = (bf16[2,4,240,128]{3,2,1,0:T(8,128)(2,1)S(1)}, bf16[2,4,240,128]{3,2,1,0:T(8,128)(2,1)S(1)}, u32[]{:S(2)}, u32[]{:S(2)}) collective-permute-start(bf16[2,4,240,128]{3,2,1,0:T(8,128)(2,1)S(1)} %collective-permute-done.12.from_right), channel_id=1, source_target_pairs={{0,7},{1,0},{2,1},{3,2},{4,3},{5,4},{6,5},{7,6},{8,15},{9,8},{10,9... | collective-permute-start | bytes 1474568 | tf_op jit(solution)/shard_map/ppermute | solution.py:392
  359.8 22.4 %collective-permute-start.6 = (bf16[2,4,240,128]{3,2,1,0:T(8,128)(2,1)S(1)}, bf16[2,4,240,128]{3,2,1,0:T(8,128)(2,1)S(1)}, u32[]{:S(2)}, u32[]{:S(2)}) collective-permute-start(bf16[2,4,240,128]{3,2,1,0:T(8,128)(2,1)S(1)} %collective-permute-done.5.from_left), channel_id=1, source_target_pairs={{0,1},{1,2},{2,3},{3,4},{4,5},{5,6},{6,7},{7,0},{8,9},{9,10},{10,1... | collective-permute-start | bytes 1474568 | tf_op jit(solution)/shard_map/ppermute | solution.py:392
  (27 other events, 231.8 us)

commit v2 on v1

--- a/solution.py
+++ b/solution.py
@@ -12,6 +12,7 @@
 TILE = 256
 SLOTS = 6
 GAP = 2
+GATHER_FROM = (7, 9, 10, 17)
 
 
 def dot(a, b):
@@ -24,6 +25,9 @@
 
 def scale_of(wide):
     return lax.rsqrt(jnp.mean(wide * wide, -1, keepdims=True) + 1e-6)
+
+
+FLAGS = set()
 
 
 class Sizes:
@@ -32,6 +36,7 @@
         self.tokens, self.d = x.shape[1:]
         self.layers, _, self.ff = w_gate.shape
         self.units = self.ff // TILE
+        self.part = self.units // 2
         self.rows = self.d // self.n
         self.down = TILE // 2 // self.n
         self.halves, self.fifths = TILE // LANES, self.d // LANES
@@ -39,9 +44,9 @@
 
 
 def step_kernel(s, x_hbm, dy_hbm, wg_hbm, wu_hbm, wd_hbm, *refs):
-    (own_x, own_y), refs = (refs[0:2], refs[2:4]), refs[4:]
-    (wg, wu, wd, xh, a, a_t, dh, dh_t, dg, du, hid, own, got, final, gs, us, ds, hs, ps) = refs[:19]
-    (load_sem, w_sem, send_sem, recv_sem, out_sem) = refs[19:]
+    (near_x, near_y, all_x), refs = (refs[0:2], refs[2:4], refs[4:6]), refs[6:]
+    (wg, wu, wd, xh, a, a_t, dh, dh_t, dg, du, hid, own, got, final, gathered, gs, us, ds, hs, ps, first_in, second_in) = refs[:22]
+    (load_sem, w_sem, send_sem, recv_sem, out_sem, gather_send, gather_recv) = refs[22:]
     me = lax.axis_index("dp")
     right, left = lax.rem(me + 1, s.n), lax.rem(me + s.n - 1, s.n)
     towards = (right, left)
@@ -50,14 +55,19 @@
     for neighbour in towards:
         pl.semaphore_signal(barrier, inc=1, device_id={"dp": neighbour}, device_id_type=pl.DeviceIdType.MESH)
 
+    small = TILE
     first = [
-        pltpu.make_async_copy(x_hbm.at[0], xh, load_sem.at[0]),
+        pltpu.make_async_copy(x_hbm.at[0, pl.ds(0, small)], xh.at[pl.ds(0, small)], load_sem.at[0]),
         pltpu.make_async_copy(wg_hbm.at[0], dg.at[pl.ds(0, s.d)], load_sem.at[1]),
         pltpu.make_async_copy(wu_hbm.at[0], dg.at[pl.ds(s.d, s.d)], load_sem.at[2]),
+    ]
+    rest = s.tokens - small
+    second = [
         pltpu.make_async_copy(wd_hbm.at[0], du.at[:, pl.ds(0, s.d)], load_sem.at[3]),
+        pltpu.make_async_copy(dy_hbm.at[0], dh, load_sem.at[4]),
+        pltpu.make_async_copy(x_hbm.at[0, pl.ds(small, rest)], xh.at[pl.ds(small, rest)], load_sem.at[8]),
     ]
-    second = [
-        pltpu.make_async_copy(dy_hbm.at[0], dh, load_sem.at[4]),
+    third = [
         pltpu.make_async_copy(wg_hbm.at[1], wg, load_sem.at[5]),
         pltpu.make_async_copy(wu_hbm.at[1], wu, load_sem.at[6]),
         pltpu.make_async_copy(wd_hbm.at[1], wd, load_sem.at[7]),
@@ -68,35 +78,56 @@
         copy.wait()
     for copy in second:
         copy.start()
-    second[0].wait()
-
-    small = TILE
+
+    blocks = s.tokens // small
+
+    def norm(block):
+        for r in range(0, small, 32):
+            part = pl.ds(block * small + r, 32)
+            wide = xh[part, :].astype(F32)
+            normed = (wide * scale_of(wide)).astype(BF16)
+            a[0, part, :] = normed
+            first_in[pl.ds(r, 32), :] = normed
+
+    def finish(block, ready):
+        for r in range(0, small, 32):
+            part = pl.ds(block * small + r, 32)
+            wide = xh[part, :].astype(F32)
+            h = (wide + ps[0, pl.ds(r, 32), :].astype(BF16).astype(F32)).astype(BF16).astype(F32)
+            h = jnp.where(ready, h, wide)
+            xh[part, :] = h.astype(BF16)
+            normed = (h * scale_of(h)).astype(BF16)
+            a[1, part, :] = normed
+            second_in[pl.ds(r, 32), :] = normed
+        a_t[:, pl.ds(pl.multiple_of(block * small, small), small)] = second_in[...].T
 
     def forward(block, carry):
-        rows = pl.ds(pl.multiple_of(block * small, small), small)
-        wide = xh[rows, :].astype(F32)
-        normed = (wide * scale_of(wide)).astype(BF16)
-        a[0, rows, :] = normed
+        finish(jnp.maximum(block - 1, 0), block > 0)
         for j in range(s.units):
             cols = pl.ds(j * TILE, TILE)
-            gs[j % 2] = dot(normed, dg[pl.ds(0, s.d), cols])
-            us[j % 2] = dot(normed, dg[pl.ds(s.d, s.d), cols])
+            gs[j % 2] = dot(first_in[...], dg[pl.ds(0, s.d), cols])
+            us[j % 2] = dot(first_in[...], dg[pl.ds(s.d, s.d), cols])
             for r in range(0, small, 32):
                 g = gs[j % 2, pl.ds(r, 32), :]
                 hs[pl.ds(r, 32), cols] = (g * jax.nn.sigmoid(g) * us[j % 2, pl.ds(r, 32), :]).astype(BF16)
+
+        @pl.when(block == 0)
+        def _():
+            for copy in second:
+                copy.wait()
+            for copy in third:
+                copy.start()
+
         ps[0] = dot(hs[...], du[:, pl.ds(0, s.d)])
-        for r in range(0, small, 32):
-            part = pl.ds(block * small + r, 32)
-            h = (xh[part, :].astype(F32) + ps[0, pl.ds(r, 32), :].astype(BF16).astype(F32)).astype(BF16)
-            xh[part, :] = h
-            wide = h.astype(F32)
-            a[1, part, :] = (wide * scale_of(wide)).astype(BF16)
-        a_t[:, rows] = a[1, rows, :].T
+        rows = pl.ds(pl.multiple_of(block * small, small), small)
         dh_t[:, rows] = dh[rows, :].T
+        norm(jnp.minimum(block + 1, blocks - 1))
         return carry
 
-    lax.fori_loop(0, s.tokens // small, forward, 0)
-    for copy in second[1:]:
+    norm(0)
+    lax.fori_loop(0, blocks, forward, 0)
+    finish(blocks - 1, True)
+    for copy in third:
         copy.wait()
     pl.semaphore_wait(barrier, 2)
 
@@ -192,11 +223,38 @@
                     if number < s.n - 1:
                         own[slot, way, chunk_of(way, number)] = total
                     else:
-                        final[lax.select(u < late, 1, 0), lax.select(u < late, u, u - late), way] = total
+                        unit = lax.select(u < late, u, u - late + s.units)
+                        final[lax.div(unit, s.part), way, lax.rem(unit, s.part)] = total
                     before.wait_send()
             if number < s.n - 1:
                 for way in range(2):
                     send(u, number, way).start()
+
+    def spread(u, number):
+        @pl.when((u >= 0) & (u < s.part))
+        def _():
+            for way in range(2):
+                def copy(hop):
+                    return pltpu.make_async_remote_copy(
+                        src_ref=final.at[0, way, u] if hop == 0 else gathered.at[way, hop - 1, u],
+                        dst_ref=gathered.at[way, hop, u],
+                        send_sem=gather_send.at[u, way],
+                        recv_sem=gather_recv.at[u, hop, way],
+                        device_id={"dp": towards[way]},
+                        device_id_type=pl.DeviceIdType.MESH,
+                    )
+
+                if number > 0:
+                    copy(number - 1).wait_recv()
+                    copy(number - 1).wait_send()
+                if number < s.n - 1:
+                    copy(number).start()
+
+    def from_start(q):
+        unit = -1
+        for i, start in enumerate(GATHER_FROM):
+            unit = lax.select(q == start, i, unit)
+        return unit
 
     def period(q, carry):
         early = q < s.units
@@ -206,6 +264,7 @@
         slot = lax.rem(q, SLOTS)
         between = (q >= s.units) & (q < late)
         plan = ([(2, 2)], [(3, 4)], [(4, 6)], [(1, 1)], [(2, 3)], [(3, 5)], [(4, 7), (0, 0)])
+        spread_plan = plan
         for k in range(7):
             @pl.when(real)
             def _():
@@ -237,9 +296,34 @@
                         return carry
                     lax.fori_loop(0, s.units, fetch, 0)
 
+            if k == 0:
+                @pl.when(q == late + s.units + 1)
+                def _():
+                    for copy in outs(0):
+                        copy.start()
+
             for back, number in plan[k]:
                 hop(q - back, number)
+            for back, number in spread_plan[k]:
+                spread(from_start(q - back), number)
         return carry
+
+    def outs(last):
+        pairs, before = [], s.part - 1
+        for way in range(2):
+            if last:
+                pairs += [
+                    (gathered.at[way, :, before], all_x[way].at[pl.ds(1, s.n - 1), before]),
+                    (final.at[3, way], near_y[way].at[0]),
+                ]
+            else:
+                pairs += [
+                    (final.at[0, way], all_x[way].at[0]),
+                    (gathered.at[way, :, pl.ds(0, before)], all_x[way].at[pl.ds(1, s.n - 1), pl.ds(0, before)]),
+                    (final.at[1, way], near_y[way].at[1]),
+                    (final.at[2, way], near_x[way]),
+                ]
+        return [pltpu.make_async_copy(*pair, out_sem.at[last, i]) for i, pair in enumerate(pairs)]
 
     def pieces(unit):
         cols = pl.ds(pl.multiple_of(unit * TILE, TILE), TILE)
@@ -250,28 +334,22 @@
         ]
 
     lax.fori_loop(0, late + s.units + 4, period, 0)
-
-    half = s.units // 2
-    outs = [
-        pltpu.make_async_copy(final.at[:, pl.ds(part * half, half), way], (own_x, own_y)[part][way], out_sem.at[part, way])
-        for part in range(2)
-        for way in range(2)
-    ]
-    for copy in outs:
+    for copy in outs(1):
         copy.start()
-    for copy in outs:
+    for copy in outs(0) + outs(1):
         copy.wait()
 
 
 def reduced_shards(s, x, dy, w_gate, w_up, w_down):
-    shard = jax.ShapeDtypeStruct((s.layers, s.units // 2, s.message, LANES), BF16)
+    part = (s.part, s.message, LANES)
+    shapes = [jax.ShapeDtypeStruct(lead + part, BF16) for lead in ((), (s.layers,), (s.n,)) for _ in range(2)]
     d, t, ff = s.d, s.tokens, s.ff
     any_space = pl.BlockSpec(memory_space=pl.ANY)
     out = pl.pallas_call(
         functools.partial(step_kernel, s),
-        out_shape=(shard,) * 4,
+        out_shape=shapes,
         in_specs=[any_space] * 5,
-        out_specs=(any_space,) * 4,
+        out_specs=[any_space] * 6,
         scratch_shapes=[
             pltpu.VMEM((d, ff), BF16),
             pltpu.VMEM((d, ff), BF16),
@@ -286,21 +364,26 @@
             pltpu.VMEM((t, TILE), BF16),
             pltpu.VMEM((SLOTS, 2, s.n, s.message, LANES), BF16),
             pltpu.VMEM((SLOTS, s.n - 1, 2, s.message, LANES), BF16),
-            pltpu.VMEM((s.layers, s.units, 2, s.message, LANES), BF16),
+            pltpu.VMEM((2 * s.layers, 2, *part), BF16),
+            pltpu.VMEM((2, s.n - 1, *part), BF16),
             pltpu.VMEM((2, TILE, TILE), F32),
             pltpu.VMEM((2, TILE, TILE), F32),
             pltpu.VMEM((2, TILE, TILE), BF16),
             pltpu.VMEM((TILE, ff), BF16),
             pltpu.VMEM((2, TILE, d), F32),
-            pltpu.SemaphoreType.DMA((8,)),
+            pltpu.VMEM((TILE, d), BF16),
+            pltpu.VMEM((TILE, d), BF16),
+            pltpu.SemaphoreType.DMA((9,)),
             pltpu.SemaphoreType.DMA((3, s.units)),
             pltpu.SemaphoreType.DMA((SLOTS, 2)),
             pltpu.SemaphoreType.DMA((SLOTS, s.n - 1, 2)),
-            pltpu.SemaphoreType.DMA((2, 2)),
+            pltpu.SemaphoreType.DMA((2, 8)),
+            pltpu.SemaphoreType.DMA((s.part, 2)),
+            pltpu.SemaphoreType.DMA((s.part, s.n - 1, 2)),
         ],
         compiler_params=pltpu.CompilerParams(collective_id=0, has_side_effects=True, vmem_limit_bytes=67043328),
     )(x, dy, w_gate, w_up, w_down)
-    return [out[0:2], out[2:4]]
+    return out[0:2], out[2:4], out[4:6]
 
 
 def adamw(w, m, v, g):
@@ -310,67 +393,135 @@
     return (w - 0.02 * step).astype(BF16), m, v
 
 
-def adamw_kernel(s, where_ref, from_left, from_right, *refs):
-    across, down = (refs[0:3], refs[3:6]), refs[6:9]
-    outs = refs[len(refs) - 9 :]
-    across_out, down_out = (outs[0:3], outs[3:6]), outs[6:9]
-
-    for way, message in enumerate((from_left, from_right)):
-        @pl.when(pl.program_id(0) == way)
+AHEAD = 2
+
+
+def adamw_kernel(s, items, operands, *refs):
+    messages, refs = refs[: 2 * operands], refs[2 * operands :]
+    state, refs = (refs[0:3], refs[3:6], refs[6:9]), refs[9:]
+    refs = refs[len(refs) - 24 :]
+    outs, refs = (refs[0:3], refs[3:6], refs[6:9]), refs[9:]
+    (message_in, across_in, down_in, across_out, down_out), (sem_in, sem_out) = (refs[0], refs[1:4], refs[4:7], refs[7:10], refs[10:13]), refs[13:15]
+    me = lax.axis_index("dp")
+
+    def of(field, item):
+        values = [one[field] for one in items]
+        if isinstance(item, int):
+            return values[item]
+        if len(set(values)) == 1:
+            return values[0]
+        out = values[-1]
+        for i in reversed(range(len(values) - 1)):
+            out = jnp.where(item == i, values[i], out)
+        return out
+
+    def places(item, way, group):
+        layer, part, away = of(0, item), of(1, item), of(2, item)
+        chunk = lax.rem(me + (s.n - away if way == 0 else away), s.n)
+        rows = pl.ds(pl.multiple_of(chunk * s.rows, s.rows), s.rows)
+        cols = pl.ds(pl.multiple_of(part * (s.part * TILE), s.part * TILE), s.part * TILE)
+        units = pl.ds(part * s.part, s.part)
+        return [ref.at[layer, rows, cols] for ref in group[way]] + [ref.at[layer, units, way, chunk] for ref in group[2]]
+
+    def loads(item, way):
+        spots = [ref.at[item, way] for ref in (*across_in, *down_in)]
+        return [
+            pltpu.make_async_copy(*pair, sem_in.at[item, way, 1 + i])
+            for i, pair in enumerate(zip(places(item, way, state), spots, strict=True))
+        ]
+
+    def message_load(item, way, which):
+        return pltpu.make_async_copy(messages[2 * which + way].at[of(4, item)], message_in.at[item, way], sem_in.at[item, way, 0])
+
+    def stores(item, way):
+        spots = [ref.at[item, way] for ref in (*across_out, *down_out)]
+        return [
+            pltpu.make_async_copy(*pair, sem_out.at[item, way, i])
+            for i, pair in enumerate(zip(spots, places(item, way, outs), strict=True))
+        ]
+
+    def fetch(item, carry=0):
+        for way in range(2):
+            for which in range(operands):
+                @pl.when(of(3, item) == which)
+                def _():
+                    message_load(item, way, which).start()
+            for copy in loads(item, way):
+                copy.start()
+        return carry
+
+    def work(item, carry):
+        @pl.when(item + AHEAD < len(items))
         def _():
+            fetch(item + AHEAD)
+
+        for way in range(2):
+            message_load(item, way, 0).wait()
+            for copy in loads(item, way):
+                copy.wait()
+
             def unit_step(unit, carry):
                 for half in range(s.halves):
-                    g = message[0, unit, pl.ds(half * s.rows, s.rows), :].astype(F32)
+                    g = message_in[item, way, unit, pl.ds(half * s.rows, s.rows), :].astype(F32)
                     cols = pl.ds(pl.multiple_of(unit * TILE + half * LANES, LANES), LANES)
-                    w, m, v = (ref[0, :, cols] for ref in across[way])
+                    w, m, v = (ref[item, way, :, cols] for ref in across_in)
                     new = adamw(w.astype(F32), m, v, g)
-                    for ref, value in zip(across_out[way], new, strict=True):
-                        ref[0, :, cols] = value
+                    for ref, value in zip(across_out, new, strict=True):
+                        ref[item, way, :, cols] = value
                 for fifth in range(s.fifths):
-                    g = message[0, unit, pl.ds(s.halves * s.rows + fifth * s.down, s.down), :].astype(F32)
+                    g = message_in[item, way, unit, pl.ds(s.halves * s.rows + fifth * s.down, s.down), :].astype(F32)
                     cols = pl.ds(fifth * LANES, LANES)
-                    w, m, v = (ref[0, unit, 0, 0, :, cols] for ref in down)
+                    w, m, v = (ref[item, way, unit, :, cols] for ref in down_in)
                     new = adamw(w.astype(F32), m, v, g)
                     for ref, value in zip(down_out, new, strict=True):
-                        ref[0, unit, 0, 0, :, cols] = value
+                        ref[item, way, unit, :, cols] = value
                 return carry
 
-            lax.fori_loop(0, s.units // 2, unit_step, 0)
-
-
-def adamw_on(s, part, hop, messages, state, so_far):
-    me = lax.axis_index("dp")
-    where = jnp.stack([lax.rem(me + s.n - hop, s.n), lax.rem(me + hop, s.n)]).astype(jnp.int32)
-    half = s.units // 2
-    last = s.layers - 1
-    spec_across = (
-        pl.BlockSpec((1, s.rows, half * TILE), lambda way, layer, at: (jnp.where(way == 0, layer, last), at[0], part)),
-        pl.BlockSpec((1, s.rows, half * TILE), lambda way, layer, at: (jnp.where(way == 0, 0, layer), at[1], part)),
-    )
-    spec_down = pl.BlockSpec((1, half, 1, 1, s.down, s.d), lambda way, layer, at: (layer, part, way, at[way], 0, 0))
-    spec_message = (
-        pl.BlockSpec((1, half, s.message, LANES), lambda way, layer, at: (jnp.where(way == 0, layer, last), 0, 0, 0)),
-        pl.BlockSpec((1, half, s.message, LANES), lambda way, layer, at: (jnp.where(way == 0, 0, layer), 0, 0, 0)),
-    )
-    specs = [spec_across[0]] * 3 + [spec_across[1]] * 3 + [spec_down] * 3
+            lax.fori_loop(0, s.part, unit_step, 0)
+            for copy in stores(item, way):
+                copy.start()
+        return carry
+
+    def drain(item, carry):
+        for way in range(2):
+            for copy in stores(item, way):
+                copy.wait()
+        return carry
+
+    for item in range(min(AHEAD, len(items))):
+        fetch(item)
+    lax.fori_loop(0, len(items), work, 0)
+    lax.fori_loop(0, len(items), drain, 0)
+
+
+def adamw_on(s, items, messages, state, so_far):
     flat = [one for group in state for one in group]
     shapes = [jax.ShapeDtypeStruct(one.shape, one.dtype) for one in flat]
-    in_specs = list(spec_message) + specs
-    args = [*messages, *flat]
+    args = [one for pair in messages for one in pair] + flat
     aliases = {}
     if so_far is not None:
-        aliases = {1 + len(args) + i: i for i in range(9)}
+        aliases = {len(args) + i: i for i in range(9)}
         args += so_far
-        in_specs += [pl.BlockSpec(memory_space=pl.ANY)] * 9
-    numbers = 2 * s.layers * half * s.message * LANES
+    count = (len(items), 2)
+    across, down = (*count, s.rows, s.part * TILE), (*count, s.part, s.down, s.d)
+    types = (BF16, F32, F32)
+    buffers = [pltpu.VMEM(shape, dtype) for shape in (across, down) for dtype in types]
+    numbers = 2 * len(items) * s.part * s.message * LANES
+    any_space = pl.BlockSpec(memory_space=pl.ANY)
     return list(
         pl.pallas_call(
-            functools.partial(adamw_kernel, s),
+            functools.partial(adamw_kernel, s, items, len(messages)),
             out_shape=shapes,
-            grid_spec=pltpu.PrefetchScalarGridSpec(num_scalar_prefetch=1, grid=(2, s.layers), in_specs=in_specs, out_specs=specs),
+            in_specs=[any_space] * len(args),
+            out_specs=[any_space] * 9,
             input_output_aliases=aliases,
+            scratch_shapes=[pltpu.VMEM((*count, s.part, s.message, LANES), BF16)]
+            + buffers
+            + buffers
+            + [pltpu.SemaphoreType.DMA((*count, 7)), pltpu.SemaphoreType.DMA((*count, 6))],
+            compiler_params=pltpu.CompilerParams(vmem_limit_bytes=67043328),
             cost_estimate=pl.CostEstimate(flops=numbers * 20 * 1000, bytes_accessed=numbers * 22, transcendentals=numbers),
-        )(where, *args)
+        )(*args)
     )
 
 
@@ -380,18 +531,32 @@
     def step(x, dy, *arrays):
         weights, m, v = (arrays[i : i + 3] for i in (0, 3, 6))
         s = Sizes(mesh, x, weights[0])
-        halves = reduced_shards(s, x, dy, *weights)
+        near_x, near_y, all_x = reduced_shards(s, x, dy, *weights)
+        near_x = [one[None] for one in near_x]
         by_chunk = (s.layers, s.units, 2, s.n, s.down, s.d)
         state = [list(group) for group in zip(weights, m, v, strict=True)]
         state[2] = [one.reshape(by_chunk) for one in state[2]]
         rings = ([(i, (i + 1) % n) for i in range(n)], [(i, (i - 1) % n) for i in range(n)])
-        out = None
+
+        def shift(pair):
+            return [lax.ppermute(one, "dp", ring) for one, ring in zip(pair, rings, strict=True)]
+
+        out, now_x, now_y = None, near_x, near_y
         for hop in range(n):
-            now = halves
+            this_x, this_y = now_x, now_y
+            y_items = [(0, 1, hop, 1, 0), (1, 1, hop, 1, 1)]
             if hop < n - 1:
-                halves = [[lax.ppermute(one, "dp", ring) for one, ring in zip(pair, rings, strict=True)] for pair in halves]
-            for part in range(2):
-                out = adamw_on(s, part, hop, now[part], state, out)
+                if hop > 0:
+                    this_y, _ = lax.optimization_barrier((this_y, before))
+                    this_x, _ = lax.optimization_barrier((this_x, this_y))
+                before = this_x
+                now_y, now_x = shift(this_y), shift(this_x)
+                here = [(1, 0, away, 0, away) for away in ((0, n - 1) if hop == 0 else (hop,))]
+                out = adamw_on(s, [*here, *y_items, (0, 0, hop, 2, 0)], [all_x, this_y, this_x], state, out)
+            else:
+                y_items = [(layer, part, away, 0, place) for layer, part, away, _, place in y_items]
+                out = adamw_on(s, y_items, [this_y], state, out)
+                out = adamw_on(s, [(0, 0, hop, 0, 0)], [this_x], state, out)
         out[6:9] = [one.reshape(weights[2].shape) for one in out[6:9]]
         return tuple(out[3 * which + i] for i in range(3) for which in range(3))
 

time: 392 us -> 365 us (0.931)
  Pallas kernels: 336 us -> 316 us
  other arithmetic: 4.81 us -> 0 us
    pallas_call x17 -> x10, Pallas kernels: 336 us -> 316 us  [the longest x1 242 us: reduced_shards(): pl.pallas_call(functools.partial(step_kernel, s), out_shape=shapes, in_sp...]
    another operation x8 -> x0, other arithmetic: 4.81 us -> none  [adamw_on(): jnp.stack([lax.rem(me + s.n - hop, s.n), lax.rem(me + hop, s.n)])]
  transfers between devices with their start and end apart: 28 -> 28, of which waited for: 1 -> 1; matrix products, arithmetic and copies ran while one was open for 1% -> 0% of each run, Pallas kernels for 27% -> 19%
where the time goes in v2:
time: 365 us
  Pallas kernels  316 us (87%)
  starting transfers between devices  46.3 us (13%)
    pallas_call x1, Pallas kernels, reduced_shards(): pl.pallas_call(functools.partial(step_kernel, s), out_shape=shapes, in_sp...  242 us
    pallas_call x9, Pallas kernels, adamw_on(): pl.pallas_call(functools.partial(adamw_kernel, s, items, len(messages)),...  73.9 us
    ppermute x28, starting transfers between devices, shift(): lax.ppermute(one, 'dp', ring)  46.3 us
  transfers between devices with their start and end apart: 28, of which 1 were waited for; matrix products, arithmetic and copies ran while one was open for 0% of the time, Pallas kernels for 19%

profile of v2, /device:TPU:22, one launch (start us, length us, event | category | flops | bytes accessed | tf_op | source)
XLA Modules:
  0.0 364.6 jit_solution(10285817578646355016)
XLA Ops:
  0.6 242.1 %shard_map.178 = (bf16[4,240,128]{2,1,0:T(8,128)(2,1)}, bf16[4,240,128]{2,1,0:T(8,128)(2,1)}, bf16[2,4,240,128]{3,2,1,0:T(8,128)(2,1)}, bf16[2,4,240,128]{3,2,1,...) custom-call(bf16[1,2048,640]{2,1,0:T(8,128)(2,1)} %x_hbm.1, ...), custom_call_target="tpu_custom_call" | custom-call | tf_op jit(solution)/shard_map/pallas_call | solution.py:348
  243.0 3.1 collective-permute-start.3
  246.1 3.2 collective-permute-start.1
  249.4 11.4 %shard_map.179 = (bf16[2,640,2048]{2,1,0:T(8,128)(2,1)}, f32[2,640,2048]{2,1,0:T(8,128)}, f32[2,640,2048]{2,1,0:T(8,128)}, bf16[2,640,2048]{2,1,0:T(8,128)(2,1)}...) custom-call(bf16[8,4,240,128]{3,2,1,0:T(8,128)(2,1)} %get-tuple-elem, ...), custom_call_target="tpu_custom_call" | custom-call | flops 24576000000 | bytes 27033600 | tf_op jit(solution)/shard_map/pallas_call | solution.py:512
  260.9 3.2 collective-permute-start.7
  264.1 3.2 collective-permute-start.5
  267.3 9.0 %shard_map.180 = (bf16[2,640,2048]{2,1,0:T(8,128)(2,1)}, f32[2,640,2048]{2,1,0:T(8,128)}, f32[2,640,2048]{2,1,0:T(8,128)}, bf16[2,640,2048]{2,1,0:T(8,128)(2,1)}...) custom-call(bf16[8,4,240,128]{3,2,1,0:T(8,128)(2,1)} %get-tuple-elem, ...), custom_call_target="tpu_custom_call", output_to_operand_aliasing={{0}: (15, {}), {1}: (16, {}), {2}: (17, {}), {3}: (18, {}),... | custom-call | flops 19660800000 | bytes 21626880 | tf_op jit(solution)/shard_map/pallas_call | solution.py:512
  276.5 3.2 collective-permute-start.11
  279.8 3.2 collective-permute-start.9
  283.0 9.0 %shard_map.181 = (bf16[2,640,2048]{2,1,0:T(8,128)(2,1)}, f32[2,640,2048]{2,1,0:T(8,128)}, f32[2,640,2048]{2,1,0:T(8,128)}, bf16[2,640,2048]{2,1,0:T(8,128)(2,1)}...) custom-call(bf16[8,4,240,128]{3,2,1,0:T(8,128)(2,1)} %get-tuple-elem, ...), custom_call_target="tpu_custom_call", output_to_operand_aliasing={{0}: (15, {}), {1}: (16, {}), {2}: (17, {}), {3}: (18, {}),... | custom-call | flops 19660800000 | bytes 21626880 | tf_op jit(solution)/shard_map/pallas_call | solution.py:512
  292.2 3.2 collective-permute-start.15
  295.4 3.2 collective-permute-start.13
  298.6 9.0 %shard_map.182 = (bf16[2,640,2048]{2,1,0:T(8,128)(2,1)}, f32[2,640,2048]{2,1,0:T(8,128)}, f32[2,640,2048]{2,1,0:T(8,128)}, bf16[2,640,2048]{2,1,0:T(8,128)(2,1)}...) custom-call(bf16[8,4,240,128]{3,2,1,0:T(8,128)(2,1)} %get-tuple-elem, ...), custom_call_target="tpu_custom_call", output_to_operand_aliasing={{0}: (15, {}), {1}: (16, {}), {2}: (17, {}), {3}: (18, {}),... | custom-call | flops 19660800000 | bytes 21626880 | tf_op jit(solution)/shard_map/pallas_call | solution.py:512
  307.8 3.2 collective-permute-start.19
  311.1 3.2 collective-permute-start.17
  314.3 9.1 %shard_map.183 = (bf16[2,640,2048]{2,1,0:T(8,128)(2,1)}, f32[2,640,2048]{2,1,0:T(8,128)}, f32[2,640,2048]{2,1,0:T(8,128)}, bf16[2,640,2048]{2,1,0:T(8,128)(2,1)}...) custom-call(bf16[8,4,240,128]{3,2,1,0:T(8,128)(2,1)} %get-tuple-elem, ...), custom_call_target="tpu_custom_call", output_to_operand_aliasing={{0}: (15, {}), {1}: (16, {}), {2}: (17, {}), {3}: (18, {}),... | custom-call | flops 19660800000 | bytes 21626880 | tf_op jit(solution)/shard_map/pallas_call | solution.py:512
  323.5 3.2 collective-permute-start.23
  326.7 3.3 collective-permute-start.21
  330.1 9.0 %shard_map.184 = (bf16[2,640,2048]{2,1,0:T(8,128)(2,1)}, f32[2,640,2048]{2,1,0:T(8,128)}, f32[2,640,2048]{2,1,0:T(8,128)}, bf16[2,640,2048]{2,1,0:T(8,128)(2,1)}...) custom-call(bf16[8,4,240,128]{3,2,1,0:T(8,128)(2,1)} %get-tuple-elem, ...), custom_call_target="tpu_custom_call", output_to_operand_aliasing={{0}: (15, {}), {1}: (16, {}), {2}: (17, {}), {3}: (18, {}),... | custom-call | flops 19660800000 | bytes 21626880 | tf_op jit(solution)/shard_map/pallas_call | solution.py:512
  339.3 3.2 collective-permute-start.27
  343.6 3.5 collective-permute-start.25
  347.1 9.0 %shard_map.185 = (bf16[2,640,2048]{2,1,0:T(8,128)(2,1)}, f32[2,640,2048]{2,1,0:T(8,128)}, f32[2,640,2048]{2,1,0:T(8,128)}, bf16[2,640,2048]{2,1,0:T(8,128)(2,1)}...) custom-call(bf16[8,4,240,128]{3,2,1,0:T(8,128)(2,1)} %get-tuple-elem, ...), custom_call_target="tpu_custom_call", output_to_operand_aliasing={{0}: (15, {}), {1}: (16, {}), {2}: (17, {}), {3}: (18, {}),... | custom-call | flops 19660800000 | bytes 21626880 | tf_op jit(solution)/shard_map/pallas_call | solution.py:512
  356.2 4.7 %shard_map.186 = (bf16[2,640,2048]{2,1,0:T(8,128)(2,1)}, f32[2,640,2048]{2,1,0:T(8,128)}, f32[2,640,2048]{2,1,0:T(8,128)}, bf16[2,640,2048]{2,1,0:T(8,128)(2,1)}...) custom-call(bf16[2,4,240,128]{3,2,1,0:T(8,128)(2,1)} %collective-per, ...), custom_call_target="tpu_custom_call", output_to_operand_aliasing={{0}: (11, {}), {1}: (12, {}), {2}: (13, {}), {3}: (14, {}),... | custom-call | flops 9830400000 | bytes 10813440 | tf_op jit(solution)/shard_map/pallas_call | solution.py:512
  360.9 3.4 shard_map.187
  (42 shorter events, 2.2 us)
Async XLA Ops:
  242.8 17.9 %collective-permute-start.2 = (bf16[2,4,240,128]{3,2,1,0:T(8,128)(2,1)}, bf16[2,4,240,128]{3,2,1,0:T(8,128)(2,1)}, u32[]{:S(2)}, u32[]{:S(2)}) collective-permute-start(bf16[2,4,240,128]{3,2,1,0:T(8,128)(2,1)} %get-tuple-element.122.refs_2_), channel_id=1, source_target_pairs={{0,1},{1,2},{2,3},{3,4},{4,5},{5,6},{6,7},{7,0},{8,9},{9,10},{10,1... | collective-permute-start | bytes 1474568 | tf_op jit(solution)/shard_map/ppermute | solution.py:542
  243.0 17.7 %collective-permute-start.3 = (bf16[2,4,240,128]{3,2,1,0:T(8,128)(2,1)}, bf16[2,4,240,128]{3,2,1,0:T(8,128)(2,1)}, u32[]{:S(2)}, u32[]{:S(2)}) collective-permute-start(bf16[2,4,240,128]{3,2,1,0:T(8,128)(2,1)} %get-tuple-element.123.refs_3_), channel_id=1, source_target_pairs={{0,7},{1,0},{2,1},{3,2},{4,3},{5,4},{6,5},{7,6},{8,15},{9,8},{10,9... | collective-permute-start | bytes 1474568 | tf_op jit(solution)/shard_map/ppermute | solution.py:542
  246.1 18.0 %collective-permute-start = (bf16[1,4,240,128]{3,2,1,0:T(8,128)(2,1)}, bf16[1,4,240,128]{3,2,1,0:T(8,128)(2,1)}, u32[]{:S(2)}, u32[]{:S(2)}) collective-permute-start(bf16[1,4,240,128]{3,2,1,0:T(8,128)(2,1)} %bitcast.40), channel_id=1, source_target_pairs={{0,1},{1,2},{2,3},{3,4},{4,5},{5,6},{6,7},{7,0},{8,9},{9,10},{10,1... | collective-permute-start | bytes 737288 | tf_op jit(solution)/shard_map/ppermute | solution.py:542
  246.1 18.0 %collective-permute-start.1 = (bf16[1,4,240,128]{3,2,1,0:T(8,128)(2,1)}, bf16[1,4,240,128]{3,2,1,0:T(8,128)(2,1)}, u32[]{:S(2)}, u32[]{:S(2)}) collective-permute-start(bf16[1,4,240,128]{3,2,1,0:T(8,128)(2,1)} %bitcast.38), channel_id=1, source_target_pairs={{0,7},{1,0},{2,1},{3,2},{4,3},{5,4},{6,5},{7,6},{8,15},{9,8},{10,9... | collective-permute-start | bytes 737288 | tf_op jit(solution)/shard_map/ppermute | solution.py:542
  260.7 15.6 %collective-permute-start.6 = (bf16[2,4,240,128]{3,2,1,0:T(8,128)(2,1)}, bf16[2,4,240,128]{3,2,1,0:T(8,128)(2,1)}, u32[]{:S(2)}, u32[]{:S(2)}) collective-permute-start(bf16[2,4,240,128]{3,2,1,0:T(8,128)(2,1)} %collective-permute-done.2.refs_2_), channel_id=1, source_target_pairs={{0,1},{1,2},{2,3},{3,4},{4,5},{5,6},{6,7},{7,0},{8,9},{9,10},{10,1... | collective-permute-start | bytes 1474568 | tf_op jit(solution)/shard_map/ppermute | solution.py:542
  264.1 15.7 %collective-permute-start.4 = (bf16[1,4,240,128]{3,2,1,0:T(8,128)(2,1)}, bf16[1,4,240,128]{3,2,1,0:T(8,128)(2,1)}, u32[]{:S(2)}, u32[]{:S(2)}) collective-permute-start(bf16[1,4,240,128]{3,2,1,0:T(8,128)(2,1)} %collective-permute-done.refs_4_), channel_id=1, source_target_pairs={{0,1},{1,2},{2,3},{3,4},{4,5},{5,6},{6,7},{7,0},{8,9},{9,10},{10,1... | collective-permute-start | bytes 737288 | tf_op jit(solution)/shard_map/ppermute | solution.py:542
  264.1 15.6 %collective-permute-start.5 = (bf16[1,4,240,128]{3,2,1,0:T(8,128)(2,1)}, bf16[1,4,240,128]{3,2,1,0:T(8,128)(2,1)}, u32[]{:S(2)}, u32[]{:S(2)}) collective-permute-start(bf16[1,4,240,128]{3,2,1,0:T(8,128)(2,1)} %collective-permute-done.1.refs_5_), channel_id=1, source_target_pairs={{0,7},{1,0},{2,1},{3,2},{4,3},{5,4},{6,5},{7,6},{8,15},{9,8},{10,9... | collective-permute-start | bytes 737288 | tf_op jit(solution)/shard_map/ppermute | solution.py:542
  276.4 15.6 %collective-permute-start.10 = (bf16[2,4,240,128]{3,2,1,0:T(8,128)(2,1)}, bf16[2,4,240,128]{3,2,1,0:T(8,128)(2,1)}, u32[]{:S(2)}, u32[]{:S(2)}) collective-permute-start(bf16[2,4,240,128]{3,2,1,0:T(8,128)(2,1)} %collective-permute-done.6.refs_2_), channel_id=1, source_target_pairs={{0,1},{1,2},{2,3},{3,4},{4,5},{5,6},{6,7},{7,0},{8,9},{9,10},{10,1... | collective-permute-start | bytes 1474568 | tf_op jit(solution)/shard_map/ppermute | solution.py:542
  279.7 15.7 %collective-permute-start.8 = (bf16[1,4,240,128]{3,2,1,0:T(8,128)(2,1)}, bf16[1,4,240,128]{3,2,1,0:T(8,128)(2,1)}, u32[]{:S(2)}, u32[]{:S(2)}) collective-permute-start(bf16[1,4,240,128]{3,2,1,0:T(8,128)(2,1)} %collective-permute-done.4.refs_4_), channel_id=1, source_target_pairs={{0,1},{1,2},{2,3},{3,4},{4,5},{5,6},{6,7},{7,0},{8,9},{9,10},{10,1... | collective-permute-start | bytes 737288 | tf_op jit(solution)/shard_map/ppermute | solution.py:542
  279.8 15.6 %collective-permute-start.9 = (bf16[1,4,240,128]{3,2,1,0:T(8,128)(2,1)}, bf16[1,4,240,128]{3,2,1,0:T(8,128)(2,1)}, u32[]{:S(2)}, u32[]{:S(2)}) collective-permute-start(bf16[1,4,240,128]{3,2,1,0:T(8,128)(2,1)} %collective-permute-done.5.refs_5_), channel_id=1, source_target_pairs={{0,7},{1,0},{2,1},{3,2},{4,3},{5,4},{6,5},{7,6},{8,15},{9,8},{10,9... | collective-permute-start | bytes 737288 | tf_op jit(solution)/shard_map/ppermute | solution.py:542
  292.1 15.6 %collective-permute-start.14 = (bf16[2,4,240,128]{3,2,1,0:T(8,128)(2,1)}, bf16[2,4,240,128]{3,2,1,0:T(8,128)(2,1)}, u32[]{:S(2)}, u32[]{:S(2)}) collective-permute-start(bf16[2,4,240,128]{3,2,1,0:T(8,128)(2,1)} %collective-permute-done.10.refs_2_), channel_id=1, source_target_pairs={{0,1},{1,2},{2,3},{3,4},{4,5},{5,6},{6,7},{7,0},{8,9},{9,10},{10,1... | collective-permute-start | bytes 1474568 | tf_op jit(solution)/shard_map/ppermute | solution.py:542
  295.4 15.7 %collective-permute-start.12 = (bf16[1,4,240,128]{3,2,1,0:T(8,128)(2,1)}, bf16[1,4,240,128]{3,2,1,0:T(8,128)(2,1)}, u32[]{:S(2)}, u32[]{:S(2)}) collective-permute-start(bf16[1,4,240,128]{3,2,1,0:T(8,128)(2,1)} %collective-permute-done.8.refs_4_), channel_id=1, source_target_pairs={{0,1},{1,2},{2,3},{3,4},{4,5},{5,6},{6,7},{7,0},{8,9},{9,10},{10,1... | collective-permute-start | bytes 737288 | tf_op jit(solution)/shard_map/ppermute | solution.py:542
  295.4 15.6 %collective-permute-start.13 = (bf16[1,4,240,128]{3,2,1,0:T(8,128)(2,1)}, bf16[1,4,240,128]{3,2,1,0:T(8,128)(2,1)}, u32[]{:S(2)}, u32[]{:S(2)}) collective-permute-start(bf16[1,4,240,128]{3,2,1,0:T(8,128)(2,1)} %collective-permute-done.9.refs_5_), channel_id=1, source_target_pairs={{0,7},{1,0},{2,1},{3,2},{4,3},{5,4},{6,5},{7,6},{8,15},{9,8},{10,9... | collective-permute-start | bytes 737288 | tf_op jit(solution)/shard_map/ppermute | solution.py:542
  307.7 15.7 %collective-permute-start.18 = (bf16[2,4,240,128]{3,2,1,0:T(8,128)(2,1)}, bf16[2,4,240,128]{3,2,1,0:T(8,128)(2,1)}, u32[]{:S(2)}, u32[]{:S(2)}) collective-permute-start(bf16[2,4,240,128]{3,2,1,0:T(8,128)(2,1)} %collective-permute-done.14.refs_2_), channel_id=1, source_target_pairs={{0,1},{1,2},{2,3},{3,4},{4,5},{5,6},{6,7},{7,0},{8,9},{9,10},{10,1... | collective-permute-start | bytes 1474568 | tf_op jit(solution)/shard_map/ppermute | solution.py:542
  311.1 15.7 %collective-permute-start.16 = (bf16[1,4,240,128]{3,2,1,0:T(8,128)(2,1)}, bf16[1,4,240,128]{3,2,1,0:T(8,128)(2,1)}, u32[]{:S(2)}, u32[]{:S(2)}) collective-permute-start(bf16[1,4,240,128]{3,2,1,0:T(8,128)(2,1)} %collective-permute-done.12.refs_4_), channel_id=1, source_target_pairs={{0,1},{1,2},{2,3},{3,4},{4,5},{5,6},{6,7},{7,0},{8,9},{9,10},{10,1... | collective-permute-start | bytes 737288 | tf_op jit(solution)/shard_map/ppermute | solution.py:542
  311.1 15.6 %collective-permute-start.17 = (bf16[1,4,240,128]{3,2,1,0:T(8,128)(2,1)}, bf16[1,4,240,128]{3,2,1,0:T(8,128)(2,1)}, u32[]{:S(2)}, u32[]{:S(2)}) collective-permute-start(bf16[1,4,240,128]{3,2,1,0:T(8,128)(2,1)} %collective-permute-done.13.refs_5_), channel_id=1, source_target_pairs={{0,7},{1,0},{2,1},{3,2},{4,3},{5,4},{6,5},{7,6},{8,15},{9,8},{10,9... | collective-permute-start | bytes 737288 | tf_op jit(solution)/shard_map/ppermute | solution.py:542
  323.4 15.7 %collective-permute-start.22 = (bf16[2,4,240,128]{3,2,1,0:T(8,128)(2,1)}, bf16[2,4,240,128]{3,2,1,0:T(8,128)(2,1)}, u32[]{:S(2)}, u32[]{:S(2)}) collective-permute-start(bf16[2,4,240,128]{3,2,1,0:T(8,128)(2,1)} %collective-permute-done.18.refs_2_), channel_id=1, source_target_pairs={{0,1},{1,2},{2,3},{3,4},{4,5},{5,6},{6,7},{7,0},{8,9},{9,10},{10,1... | collective-permute-start | bytes 1474568 | tf_op jit(solution)/shard_map/ppermute | solution.py:542
  323.5 15.6 %collective-permute-start.23 = (bf16[2,4,240,128]{3,2,1,0:T(8,128)(2,1)}, bf16[2,4,240,128]{3,2,1,0:T(8,128)(2,1)}, u32[]{:S(2)}, u32[]{:S(2)}) collective-permute-start(bf16[2,4,240,128]{3,2,1,0:T(8,128)(2,1)} %collective-permute-done.19.refs_3_), channel_id=1, source_target_pairs={{0,7},{1,0},{2,1},{3,2},{4,3},{5,4},{6,5},{7,6},{8,15},{9,8},{10,9... | collective-permute-start | bytes 1474568 | tf_op jit(solution)/shard_map/ppermute | solution.py:542
  326.7 16.9 %collective-permute-start.20 = (bf16[1,4,240,128]{3,2,1,0:T(8,128)(2,1)}, bf16[1,4,240,128]{3,2,1,0:T(8,128)(2,1)}, u32[]{:S(2)}, u32[]{:S(2)}) collective-permute-start(bf16[1,4,240,128]{3,2,1,0:T(8,128)(2,1)} %collective-permute-done.16.refs_4_), channel_id=1, source_target_pairs={{0,1},{1,2},{2,3},{3,4},{4,5},{5,6},{6,7},{7,0},{8,9},{9,10},{10,1... | collective-permute-start | bytes 737288 | tf_op jit(solution)/shard_map/ppermute | solution.py:542
  326.7 16.8 %collective-permute-start.21 = (bf16[1,4,240,128]{3,2,1,0:T(8,128)(2,1)}, bf16[1,4,240,128]{3,2,1,0:T(8,128)(2,1)}, u32[]{:S(2)}, u32[]{:S(2)}) collective-permute-start(bf16[1,4,240,128]{3,2,1,0:T(8,128)(2,1)} %collective-permute-done.17.refs_5_), channel_id=1, source_target_pairs={{0,7},{1,0},{2,1},{3,2},{4,3},{5,4},{6,5},{7,6},{8,15},{9,8},{10,9... | collective-permute-start | bytes 737288 | tf_op jit(solution)/shard_map/ppermute | solution.py:542
  339.1 17.0 %collective-permute-start.26 = (bf16[2,4,240,128]{3,2,1,0:T(8,128)(2,1)}, bf16[2,4,240,128]{3,2,1,0:T(8,128)(2,1)}, u32[]{:S(2)}, u32[]{:S(2)}) collective-permute-start(bf16[2,4,240,128]{3,2,1,0:T(8,128)(2,1)} %collective-permute-done.22.refs_2_), channel_id=1, source_target_pairs={{0,1},{1,2},{2,3},{3,4},{4,5},{5,6},{6,7},{7,0},{8,9},{9,10},{10,1... | collective-permute-start | bytes 1474568 | tf_op jit(solution)/shard_map/ppermute | solution.py:542
  339.3 16.9 %collective-permute-start.27 = (bf16[2,4,240,128]{3,2,1,0:T(8,128)(2,1)}, bf16[2,4,240,128]{3,2,1,0:T(8,128)(2,1)}, u32[]{:S(2)}, u32[]{:S(2)}) collective-permute-start(bf16[2,4,240,128]{3,2,1,0:T(8,128)(2,1)} %collective-permute-done.23.refs_3_), channel_id=1, source_target_pairs={{0,7},{1,0},{2,1},{3,2},{4,3},{5,4},{6,5},{7,6},{8,15},{9,8},{10,9... | collective-permute-start | bytes 1474568 | tf_op jit(solution)/shard_map/ppermute | solution.py:542
  343.6 17.3 %collective-permute-start.24 = (bf16[1,4,240,128]{3,2,1,0:T(8,128)(2,1)}, bf16[1,4,240,128]{3,2,1,0:T(8,128)(2,1)}, u32[]{:S(2)}, u32[]{:S(2)}) collective-permute-start(bf16[1,4,240,128]{3,2,1,0:T(8,128)(2,1)} %collective-permute-done.20.refs_4_), channel_id=1, source_target_pairs={{0,1},{1,2},{2,3},{3,4},{4,5},{5,6},{6,7},{7,0},{8,9},{9,10},{10,1... | collective-permute-start | bytes 737288 | tf_op jit(solution)/shard_map/ppermute | solution.py:542
  343.6 17.4 %collective-permute-start.25 = (bf16[1,4,240,128]{3,2,1,0:T(8,128)(2,1)}, bf16[1,4,240,128]{3,2,1,0:T(8,128)(2,1)}, u32[]{:S(2)}, u32[]{:S(2)}) collective-permute-start(bf16[1,4,240,128]{3,2,1,0:T(8,128)(2,1)} %collective-permute-done.21.refs_5_), channel_id=1, source_target_pairs={{0,7},{1,0},{2,1},{3,2},{4,3},{5,4},{6,5},{7,6},{8,15},{9,8},{10,9... | collective-permute-start | bytes 737288 | tf_op jit(solution)/shard_map/ppermute | solution.py:542
  (4 other events, 62.1 us)

commit v3 on v2

--- a/solution.py
+++ b/solution.py
@@ -10,9 +10,9 @@
 F32, BF16 = jnp.float32, jnp.bfloat16
 LANES = 128
 TILE = 256
-SLOTS = 6
+SLOTS = 4
 GAP = 2
-GATHER_FROM = (7, 9, 10, 17)
+GATHER_FROM = (6, 7, 8, 16)
 
 
 def dot(a, b):
@@ -37,6 +37,7 @@
         self.layers, _, self.ff = w_gate.shape
         self.units = self.ff // TILE
         self.part = self.units // 2
+        self.far = self.n // 2
         self.rows = self.d // self.n
         self.down = TILE // 2 // self.n
         self.halves, self.fifths = TILE // LANES, self.d // LANES
@@ -72,12 +73,9 @@
         pltpu.make_async_copy(wu_hbm.at[1], wu, load_sem.at[6]),
         pltpu.make_async_copy(wd_hbm.at[1], wd, load_sem.at[7]),
     ]
-    for copy in first:
+    for copy in first + second:
         copy.start()
-    for copy in first:
-        copy.wait()
-    for copy in second:
-        copy.start()
+    first[0].wait()
 
     blocks = s.tokens // small
 
@@ -93,7 +91,7 @@
         for r in range(0, small, 32):
             part = pl.ds(block * small + r, 32)
             wide = xh[part, :].astype(F32)
-            h = (wide + ps[0, pl.ds(r, 32), :].astype(BF16).astype(F32)).astype(BF16).astype(F32)
+            h = (wide + ps[pl.ds(r, 32), :].astype(BF16).astype(F32)).astype(BF16).astype(F32)
             h = jnp.where(ready, h, wide)
             xh[part, :] = h.astype(BF16)
             normed = (h * scale_of(h)).astype(BF16)
@@ -118,18 +116,18 @@
             for copy in third:
                 copy.start()
 
-        ps[0] = dot(hs[...], du[:, pl.ds(0, s.d)])
+        ps[...] = dot(hs[...], du[:, pl.ds(0, s.d)])
         rows = pl.ds(pl.multiple_of(block * small, small), small)
         dh_t[:, rows] = dh[rows, :].T
         norm(jnp.minimum(block + 1, blocks - 1))
         return carry
 
     norm(0)
+    for copy in first[1:]:
+        copy.wait()
     lax.fori_loop(0, blocks, forward, 0)
-    finish(blocks - 1, True)
     for copy in third:
         copy.wait()
-    pl.semaphore_wait(barrier, 2)
 
     quarter = s.tokens // 4
 
@@ -154,7 +152,7 @@
     def keep_across(slot, which, value):
         for chunk in range(s.n):
             for half in range(s.halves):
-                own[slot, which, chunk, pl.ds(half * s.rows, s.rows), :] = value[
+                own[slot, chunk, which, pl.ds(half * s.rows, s.rows), :] = value[
                     chunk * s.rows : (chunk + 1) * s.rows, half * LANES : (half + 1) * LANES
                 ]
 
@@ -172,18 +170,18 @@
             for chunk in range(s.n):
                 top = (which * s.n + chunk) * s.down
                 for fifth in range(s.fifths):
-                    own[slot, which, chunk, pl.ds(s.halves * s.rows + fifth * s.down, s.down), :] = value[
+                    own[slot, chunk, which, pl.ds(s.halves * s.rows + fifth * s.down, s.down), :] = value[
                         top : top + s.down, fifth * LANES : (fifth + 1) * LANES
                     ]
 
     def back_through_norm(block):
         at = block * TILE
         rows = pl.ds(pl.multiple_of(at, TILE), TILE)
-        ps[0] = dot_t(dg[rows, :], wg[...])
-        ps[1] = dot_t(du[rows, :], wu[...])
+        first_in[...] = dot_t(wg[...], dg[rows, :]).astype(BF16).T
+        second_in[...] = dot_t(wu[...], du[rows, :]).astype(BF16).T
         for r in range(0, TILE, 32):
             part, here = pl.ds(r, 32), pl.ds(at + r, 32)
-            by_a = (ps[0, part, :].astype(BF16).astype(F32) + ps[1, part, :].astype(BF16).astype(F32)).astype(BF16).astype(F32)
+            by_a = (first_in[part, :].astype(F32) + second_in[part, :].astype(F32)).astype(BF16).astype(F32)
             wide = xh[here, :].astype(F32)
             scale = scale_of(wide)
             by = scale * by_a - wide * (scale * scale * scale * jnp.mean(wide * by_a, -1, keepdims=True))
@@ -196,47 +194,61 @@
     def is_unit(u):
         return ((u >= 0) & (u < s.units)) | ((u >= late) & (u < late + s.units))
 
-    def chunk_of(way, hop):
-        return lax.rem(me + (s.n - 1 - hop if way == 0 else 1 + hop), s.n)
-
-    def send(u, hop, way):
+    def chunk_of(arm, hop):
+        return lax.rem(me + (s.far - hop if arm == 0 else s.n - s.far + hop), s.n)
+
+    def send(u, hop, arm, first=False):
         slot = lax.rem(u, SLOTS)
+        source, target = own.at[slot, chunk_of(arm, hop)], got.at[slot, arm, hop]
         return pltpu.make_async_remote_copy(
-            src_ref=own.at[slot, way, chunk_of(way, hop)],
-            dst_ref=got.at[slot, hop, way],
-            send_sem=send_sem.at[slot, way],
-            recv_sem=recv_sem.at[slot, hop, way],
-            device_id={"dp": towards[way]},
+            src_ref=source.at[arm] if first else source,
+            dst_ref=target.at[arm] if first else target,
+            send_sem=send_sem.at[slot, arm],
+            recv_sem=recv_sem.at[slot, arm, hop],
+            device_id={"dp": towards[arm]},
             device_id_type=pl.DeviceIdType.MESH,
         )
 
-    def hop(u, number):
+    def begin(u):
         @pl.when(is_unit(u))
         def _():
+            for arm in range(2):
+                send(u, 0, arm, first=True).start()
+
+    def join(u, number, first=False):
+        slot = lax.rem(u, SLOTS)
+        for arm in range(2):
+            before, chunk = send(u, number - 1, arm, first), chunk_of(arm, number)
+            before.wait_recv()
+            for half in [arm] if first else range(2):
+                mine = own[slot, chunk, half].astype(F32)
+                own[slot, chunk, half] = (mine + got[slot, arm, number - 1, half].astype(F32)).astype(BF16)
+            before.wait_send()
+        for arm in range(2):
+            send(u, number, arm).start()
+
+    def end(u):
+        @pl.when(is_unit(u))
+        def _():
             slot = lax.rem(u, SLOTS)
+            unit = lax.select(u < late, u, u - late + s.units)
+            for arm in range(2):
+                before = send(u, s.far - 1, arm)
+                before.wait_recv()
+                before.wait_send()
+            for half in range(2):
+                total = own[slot, me, half].astype(F32)
+                for arm in range(2):
+                    total += got[slot, arm, s.far - 1, half].astype(F32)
+                final[lax.div(unit, s.part), half, lax.rem(unit, s.part)] = total.astype(BF16)
+
+    def spread(u, number, begins=False, ends=False):
+        @pl.when((u >= 0) & (u < s.part))
+        def _():
             for way in range(2):
-                if number > 0:
-                    before = send(u, number - 1, way)
-                    before.wait_recv()
-                    mine = own[slot, way, chunk_of(way, number)].astype(F32)
-                    total = (mine + got[slot, number - 1, way].astype(F32)).astype(BF16)
-                    if number < s.n - 1:
-                        own[slot, way, chunk_of(way, number)] = total
-                    else:
-                        unit = lax.select(u < late, u, u - late + s.units)
-                        final[lax.div(unit, s.part), way, lax.rem(unit, s.part)] = total
-                    before.wait_send()
-            if number < s.n - 1:
-                for way in range(2):
-                    send(u, number, way).start()
-
-    def spread(u, number):
-        @pl.when((u >= 0) & (u < s.part))
-        def _():
-            for way in range(2):
-                def copy(hop):
+                def copy(hop, source):
                     return pltpu.make_async_remote_copy(
-                        src_ref=final.at[0, way, u] if hop == 0 else gathered.at[way, hop - 1, u],
+                        src_ref=source,
                         dst_ref=gathered.at[way, hop, u],
                         send_sem=gather_send.at[u, way],
                         recv_sem=gather_recv.at[u, hop, way],
@@ -244,17 +256,22 @@
                         device_id_type=pl.DeviceIdType.MESH,
                     )
 
-                if number > 0:
-                    copy(number - 1).wait_recv()
-                    copy(number - 1).wait_send()
-                if number < s.n - 1:
-                    copy(number).start()
+                if not begins:
+                    before = copy(number - 1, gathered.at[way, number - 1, u])
+                    before.wait_recv()
+                    before.wait_send()
+                if not ends:
+                    copy(number, final.at[0, way, u] if begins else gathered.at[way, number - 1, u]).start()
 
     def from_start(q):
         unit = -1
         for i, start in enumerate(GATHER_FROM):
             unit = lax.select(q == start, i, unit)
         return unit
+
+    finish(blocks - 1, True)
+    inner(1, 0, 0)
+    pl.semaphore_wait(barrier, 2)
 
     def period(q, carry):
         early = q < s.units
@@ -263,49 +280,66 @@
         unit = lax.select(early, q, q - late)
         slot = lax.rem(q, SLOTS)
         between = (q >= s.units) & (q < late)
-        plan = ([(2, 2)], [(3, 4)], [(4, 6)], [(1, 1)], [(2, 3)], [(3, 5)], [(4, 7), (0, 0)])
-        spread_plan = plan
-        for k in range(7):
+
+        def quarter_of(k, carry):
             @pl.when(real)
             def _():
-                if k == 0:
-                    @pl.when(q >= late)
+                for piece in range(2):
+                    @pl.when((q == late + piece) & (k == 0))
                     def _():
-                        for copy in pieces(unit):
+                        for copy in pieces(piece):
                             copy.wait()
-                if k < 4:
-                    inner(layer, unit, k)
-                elif k == 4:
-                    by_gate(unit, slot)
-                elif k == 5:
-                    by_up(unit, slot)
-                else:
-                    by_down(slot)
-
-            if k < 4:
-                @pl.when(between)
-                def _():
-                    back_through_norm((q - s.units) * 4 + k)
-
-            if k == 3:
-                @pl.when(q == late - 1)
-                def _():
-                    def fetch(piece, carry):
-                        for copy in pieces(piece):
-                            copy.start()
-                        return carry
-                    lax.fori_loop(0, s.units, fetch, 0)
-
-            if k == 0:
-                @pl.when(q == late + s.units + 1)
-                def _():
-                    for copy in outs(0):
-                        copy.start()
-
-            for back, number in plan[k]:
-                hop(q - back, number)
-            for back, number in spread_plan[k]:
-                spread(from_start(q - back), number)
+                inner(layer, unit, k)
+
+            @pl.when(between)
+            def _():
+                back_through_norm((q - s.units) * 4 + k)
+
+            @pl.when((k == 3) & is_unit(q - 1))
+            def _():
+                join(q - 1, 1, first=True)
+
+            number = 3 - lax.div(k, 2)
+            @pl.when(((k == 0) | (k == 2)) & is_unit(q - number))
+            def _():
+                join(q - number, number)
+
+            back, number = lax.select(k == 3, 1, k + 2), lax.select(k == 3, 1, 2 * k + 2)
+            spread(from_start(q - back), number)
+            return carry
+
+        lax.fori_loop(jnp.where(q == 0, 1, 0), 4, quarter_of, 0)
+
+        @pl.when(q == late - 1)
+        def _():
+            for copy in pieces(0) + pieces(1):
+                copy.start()
+
+        @pl.when(q == late + s.units)
+        def _():
+            for copy in outs(0):
+                copy.start()
+
+        @pl.when(real)
+        def _():
+            by_gate(unit, slot)
+
+        end(q - 3)
+        spread(from_start(q - 2), 3)
+
+        @pl.when(real)
+        def _():
+            by_up(unit, slot)
+
+        spread(from_start(q - 3), 5)
+
+        @pl.when(real)
+        def _():
+            by_down(slot)
+
+        begin(q)
+        spread(from_start(q - 4), s.n - 1, ends=True)
+        spread(from_start(q), 0, begins=True)
         return carry
 
     def outs(last):
@@ -325,15 +359,15 @@
                 ]
         return [pltpu.make_async_copy(*pair, out_sem.at[last, i]) for i, pair in enumerate(pairs)]
 
-    def pieces(unit):
-        cols = pl.ds(pl.multiple_of(unit * TILE, TILE), TILE)
+    def pieces(which):
+        cols = pl.ds(0, TILE) if which == 0 else pl.ds(TILE, s.ff - TILE)
         return [
-            pltpu.make_async_copy(wg_hbm.at[0, :, cols], wg.at[:, cols], w_sem.at[0, unit]),
-            pltpu.make_async_copy(wu_hbm.at[0, :, cols], wu.at[:, cols], w_sem.at[1, unit]),
-            pltpu.make_async_copy(wd_hbm.at[0, cols, :], wd.at[cols, :], w_sem.at[2, unit]),
+            pltpu.make_async_copy(wg_hbm.at[0, :, cols], wg.at[:, cols], w_sem.at[0, which]),
+            pltpu.make_async_copy(wu_hbm.at[0, :, cols], wu.at[:, cols], w_sem.at[1, which]),
+            pltpu.make_async_copy(wd_hbm.at[0, cols, :], wd.at[cols, :], w_sem.at[2, which]),
         ]
 
-    lax.fori_loop(0, late + s.units + 4, period, 0)
+    lax.fori_loop(0, max(late + s.units + 2, GATHER_FROM[-1] + 4) + 1, period, 0)
     for copy in outs(1):
         copy.start()
     for copy in outs(0) + outs(1):
@@ -362,21 +396,21 @@
             pltpu.VMEM((t, ff), BF16),
             pltpu.VMEM((t, ff), BF16),
             pltpu.VMEM((t, TILE), BF16),
-            pltpu.VMEM((SLOTS, 2, s.n, s.message, LANES), BF16),
-            pltpu.VMEM((SLOTS, s.n - 1, 2, s.message, LANES), BF16),
+            pltpu.VMEM((SLOTS, s.n, 2, s.message, LANES), BF16),
+            pltpu.VMEM((SLOTS, 2, s.far, 2, s.message, LANES), BF16),
             pltpu.VMEM((2 * s.layers, 2, *part), BF16),
             pltpu.VMEM((2, s.n - 1, *part), BF16),
             pltpu.VMEM((2, TILE, TILE), F32),
             pltpu.VMEM((2, TILE, TILE), F32),
             pltpu.VMEM((2, TILE, TILE), BF16),
             pltpu.VMEM((TILE, ff), BF16),
-            pltpu.VMEM((2, TILE, d), F32),
+            pltpu.VMEM((TILE, d), F32),
             pltpu.VMEM((TILE, d), BF16),
             pltpu.VMEM((TILE, d), BF16),
             pltpu.SemaphoreType.DMA((9,)),
-            pltpu.SemaphoreType.DMA((3, s.units)),
+            pltpu.SemaphoreType.DMA((3, 2)),
             pltpu.SemaphoreType.DMA((SLOTS, 2)),
-            pltpu.SemaphoreType.DMA((SLOTS, s.n - 1, 2)),
+            pltpu.SemaphoreType.DMA((SLOTS, 2, s.far)),
             pltpu.SemaphoreType.DMA((2, 8)),
             pltpu.SemaphoreType.DMA((s.part, 2)),
             pltpu.SemaphoreType.DMA((s.part, s.n - 1, 2)),
@@ -551,7 +585,8 @@
                     this_x, _ = lax.optimization_barrier((this_x, this_y))
                 before = this_x
                 now_y, now_x = shift(this_y), shift(this_x)
-                here = [(1, 0, away, 0, away) for away in ((0, n - 1) if hop == 0 else (hop,))]
+            here = [(1, 0, away, 0, away) for away in (range(3) if hop == 0 else [hop + 2] if hop + 2 < n else [])]
+            if here:
                 out = adamw_on(s, [*here, *y_items, (0, 0, hop, 2, 0)], [all_x, this_y, this_x], state, out)
             else:
                 y_items = [(layer, part, away, 0, place) for layer, part, away, _, place in y_items]

time: 365 us -> 359 us (0.984)
  Pallas kernels: 316 us -> 310 us
    pallas_call x1, Pallas kernels: 242 us -> 236 us  [reduced_shards(): pl.pallas_call(functools.partial(step_kernel, s), out_shape=shapes, in_sp...]
    pallas_call x9 -> x10, Pallas kernels: 73.9 us -> 74.5 us  [adamw_on(): pl.pallas_call(functools.partial(adamw_kernel, s, items, len(messages)),...]
  transfers between devices with their start and end apart: 28 -> 28, of which waited for: 1 -> 2; matrix products, arithmetic and copies ran while one was open for 0% -> 0% of each run, Pallas kernels for 19% -> 20%
where the time goes in v3:
time: 359 us
  Pallas kernels  310 us (86%)
  starting transfers between devices  45.9 us (13%)
    pallas_call x1, Pallas kernels, reduced_shards(): pl.pallas_call(functools.partial(step_kernel, s), out_shape=shapes, in_sp...  236 us
    pallas_call x10, Pallas kernels, adamw_on(): pl.pallas_call(functools.partial(adamw_kernel, s, items, len(messages)),...  74.5 us
    ppermute x28, starting transfers between devices, shift(): lax.ppermute(one, 'dp', ring)  45.9 us
  transfers between devices with their start and end apart: 28, of which 2 were waited for; matrix products, arithmetic and copies ran while one was open for 0% of the time, Pallas kernels for 20%

profile of v3, /device:TPU:22, one launch (start us, length us, event | category | flops | bytes accessed | tf_op | source)
XLA Modules:
  0.0 359.0 jit_solution(15384138657478762438)
XLA Ops:
  0.6 235.9 %shard_map.178 = (bf16[4,240,128]{2,1,0:T(8,128)(2,1)}, bf16[4,240,128]{2,1,0:T(8,128)(2,1)}, bf16[2,4,240,128]{3,2,1,0:T(8,128)(2,1)}, bf16[2,4,240,128]{3,2,1,...) custom-call(bf16[1,2048,640]{2,1,0:T(8,128)(2,1)} %x_hbm.1, ...), custom_call_target="tpu_custom_call" | custom-call | tf_op jit(solution)/shard_map/pallas_call | solution.py:382
  236.6 3.2 collective-permute-start.3
  239.8 3.2 collective-permute-start.1
  243.1 12.9 %shard_map.179 = (bf16[2,640,2048]{2,1,0:T(8,128)(2,1)}, f32[2,640,2048]{2,1,0:T(8,128)}, f32[2,640,2048]{2,1,0:T(8,128)}, bf16[2,640,2048]{2,1,0:T(8,128)(2,1)}...) custom-call(bf16[8,4,240,128]{3,2,1,0:T(8,128)(2,1)} %get-tuple-elem, ...), custom_call_target="tpu_custom_call" | custom-call | flops 29491200000 | bytes 32440320 | tf_op jit(solution)/shard_map/pallas_call | solution.py:546
  256.2 3.2 collective-permute-start.7
  259.4 3.2 collective-permute-start.5
  262.6 9.0 %shard_map.180 = (bf16[2,640,2048]{2,1,0:T(8,128)(2,1)}, f32[2,640,2048]{2,1,0:T(8,128)}, f32[2,640,2048]{2,1,0:T(8,128)}, bf16[2,640,2048]{2,1,0:T(8,128)(2,1)}...) custom-call(bf16[8,4,240,128]{3,2,1,0:T(8,128)(2,1)} %get-tuple-elem, ...), custom_call_target="tpu_custom_call", output_to_operand_aliasing={{0}: (15, {}), {1}: (16, {}), {2}: (17, {}), {3}: (18, {}),... | custom-call | flops 19660800000 | bytes 21626880 | tf_op jit(solution)/shard_map/pallas_call | solution.py:546
  271.8 3.2 collective-permute-start.11
  275.1 3.2 collective-permute-start.9
  278.3 9.0 %shard_map.181 = (bf16[2,640,2048]{2,1,0:T(8,128)(2,1)}, f32[2,640,2048]{2,1,0:T(8,128)}, f32[2,640,2048]{2,1,0:T(8,128)}, bf16[2,640,2048]{2,1,0:T(8,128)(2,1)}...) custom-call(bf16[8,4,240,128]{3,2,1,0:T(8,128)(2,1)} %get-tuple-elem, ...), custom_call_target="tpu_custom_call", output_to_operand_aliasing={{0}: (15, {}), {1}: (16, {}), {2}: (17, {}), {3}: (18, {}),... | custom-call | flops 19660800000 | bytes 21626880 | tf_op jit(solution)/shard_map/pallas_call | solution.py:546
  287.5 3.2 collective-permute-start.15
  290.7 3.2 collective-permute-start.13
  293.9 9.1 %shard_map.182 = (bf16[2,640,2048]{2,1,0:T(8,128)(2,1)}, f32[2,640,2048]{2,1,0:T(8,128)}, f32[2,640,2048]{2,1,0:T(8,128)}, bf16[2,640,2048]{2,1,0:T(8,128)(2,1)}...) custom-call(bf16[8,4,240,128]{3,2,1,0:T(8,128)(2,1)} %get-tuple-elem, ...), custom_call_target="tpu_custom_call", output_to_operand_aliasing={{0}: (15, {}), {1}: (16, {}), {2}: (17, {}), {3}: (18, {}),... | custom-call | flops 19660800000 | bytes 21626880 | tf_op jit(solution)/shard_map/pallas_call | solution.py:546
  303.1 3.2 collective-permute-start.19
  306.4 3.2 collective-permute-start.17
  309.6 9.0 %shard_map.183 = (bf16[2,640,2048]{2,1,0:T(8,128)(2,1)}, f32[2,640,2048]{2,1,0:T(8,128)}, f32[2,640,2048]{2,1,0:T(8,128)}, bf16[2,640,2048]{2,1,0:T(8,128)(2,1)}...) custom-call(bf16[8,4,240,128]{3,2,1,0:T(8,128)(2,1)} %get-tuple-elem, ...), custom_call_target="tpu_custom_call", output_to_operand_aliasing={{0}: (15, {}), {1}: (16, {}), {2}: (17, {}), {3}: (18, {}),... | custom-call | flops 19660800000 | bytes 21626880 | tf_op jit(solution)/shard_map/pallas_call | solution.py:546
  318.8 3.2 collective-permute-start.23
  322.1 3.2 collective-permute-start.21
  325.3 9.0 %shard_map.184 = (bf16[2,640,2048]{2,1,0:T(8,128)(2,1)}, f32[2,640,2048]{2,1,0:T(8,128)}, f32[2,640,2048]{2,1,0:T(8,128)}, bf16[2,640,2048]{2,1,0:T(8,128)(2,1)}...) custom-call(bf16[8,4,240,128]{3,2,1,0:T(8,128)(2,1)} %get-tuple-elem, ...), custom_call_target="tpu_custom_call", output_to_operand_aliasing={{0}: (15, {}), {1}: (16, {}), {2}: (17, {}), {3}: (18, {}),... | custom-call | flops 19660800000 | bytes 21626880 | tf_op jit(solution)/shard_map/pallas_call | solution.py:546
  339.2 3.2 collective-permute-start.25
  342.4 4.7 %shard_map.185 = (bf16[2,640,2048]{2,1,0:T(8,128)(2,1)}, f32[2,640,2048]{2,1,0:T(8,128)}, f32[2,640,2048]{2,1,0:T(8,128)}, bf16[2,640,2048]{2,1,0:T(8,128)(2,1)}...) custom-call(bf16[2,4,240,128]{3,2,1,0:T(8,128)(2,1)} %collective-per, ...), custom_call_target="tpu_custom_call", output_to_operand_aliasing={{0}: (11, {}), {1}: (12, {}), {2}: (13, {}), {3}: (14, {}),... | custom-call | flops 9830400000 | bytes 10813440 | tf_op jit(solution)/shard_map/pallas_call | solution.py:546
  347.1 3.4 shard_map.186
  350.6 4.7 %shard_map.187 = (bf16[2,640,2048]{2,1,0:T(8,128)(2,1)}, f32[2,640,2048]{2,1,0:T(8,128)}, f32[2,640,2048]{2,1,0:T(8,128)}, bf16[2,640,2048]{2,1,0:T(8,128)(2,1)}...) custom-call(bf16[2,4,240,128]{3,2,1,0:T(8,128)(2,1)} %collective-per, ...), custom_call_target="tpu_custom_call", output_to_operand_aliasing={{0}: (11, {}), {1}: (12, {}), {2}: (13, {}), {3}: (14, {}),... | custom-call | flops 9830400000 | bytes 10813440 | tf_op jit(solution)/shard_map/pallas_call | solution.py:546
  355.4 3.4 shard_map.188
  (43 shorter events, 5.7 us)
Async XLA Ops:
  236.5 19.5 %collective-permute-start.2 = (bf16[2,4,240,128]{3,2,1,0:T(8,128)(2,1)}, bf16[2,4,240,128]{3,2,1,0:T(8,128)(2,1)}, u32[]{:S(2)}, u32[]{:S(2)}) collective-permute-start(bf16[2,4,240,128]{3,2,1,0:T(8,128)(2,1)} %get-tuple-element.131.refs_2_), channel_id=1, source_target_pairs={{0,1},{1,2},{2,3},{3,4},{4,5},{5,6},{6,7},{7,0},{8,9},{9,10},{10,1... | collective-permute-start | bytes 1474568 | tf_op jit(solution)/shard_map/ppermute | solution.py:576
  236.6 19.4 %collective-permute-start.3 = (bf16[2,4,240,128]{3,2,1,0:T(8,128)(2,1)}, bf16[2,4,240,128]{3,2,1,0:T(8,128)(2,1)}, u32[]{:S(2)}, u32[]{:S(2)}) collective-permute-start(bf16[2,4,240,128]{3,2,1,0:T(8,128)(2,1)} %get-tuple-element.132.refs_3_), channel_id=1, source_target_pairs={{0,7},{1,0},{2,1},{3,2},{4,3},{5,4},{6,5},{7,6},{8,15},{9,8},{10,9... | collective-permute-start | bytes 1474568 | tf_op jit(solution)/shard_map/ppermute | solution.py:576
  239.8 19.5 %collective-permute-start = (bf16[1,4,240,128]{3,2,1,0:T(8,128)(2,1)}, bf16[1,4,240,128]{3,2,1,0:T(8,128)(2,1)}, u32[]{:S(2)}, u32[]{:S(2)}) collective-permute-start(bf16[1,4,240,128]{3,2,1,0:T(8,128)(2,1)} %bitcast.43), channel_id=1, source_target_pairs={{0,1},{1,2},{2,3},{3,4},{4,5},{5,6},{6,7},{7,0},{8,9},{9,10},{10,1... | collective-permute-start | bytes 737288 | tf_op jit(solution)/shard_map/ppermute | solution.py:576
  239.8 19.5 %collective-permute-start.1 = (bf16[1,4,240,128]{3,2,1,0:T(8,128)(2,1)}, bf16[1,4,240,128]{3,2,1,0:T(8,128)(2,1)}, u32[]{:S(2)}, u32[]{:S(2)}) collective-permute-start(bf16[1,4,240,128]{3,2,1,0:T(8,128)(2,1)} %bitcast.41), channel_id=1, source_target_pairs={{0,7},{1,0},{2,1},{3,2},{4,3},{5,4},{6,5},{7,6},{8,15},{9,8},{10,9... | collective-permute-start | bytes 737288 | tf_op jit(solution)/shard_map/ppermute | solution.py:576
  256.0 15.6 %collective-permute-start.6 = (bf16[2,4,240,128]{3,2,1,0:T(8,128)(2,1)}, bf16[2,4,240,128]{3,2,1,0:T(8,128)(2,1)}, u32[]{:S(2)}, u32[]{:S(2)}) collective-permute-start(bf16[2,4,240,128]{3,2,1,0:T(8,128)(2,1)} %collective-permute-done.2.refs_2_), channel_id=1, source_target_pairs={{0,1},{1,2},{2,3},{3,4},{4,5},{5,6},{6,7},{7,0},{8,9},{9,10},{10,1... | collective-permute-start | bytes 1474568 | tf_op jit(solution)/shard_map/ppermute | solution.py:576
  259.4 15.7 %collective-permute-start.4 = (bf16[1,4,240,128]{3,2,1,0:T(8,128)(2,1)}, bf16[1,4,240,128]{3,2,1,0:T(8,128)(2,1)}, u32[]{:S(2)}, u32[]{:S(2)}) collective-permute-start(bf16[1,4,240,128]{3,2,1,0:T(8,128)(2,1)} %collective-permute-done.refs_4_), channel_id=1, source_target_pairs={{0,1},{1,2},{2,3},{3,4},{4,5},{5,6},{6,7},{7,0},{8,9},{9,10},{10,1... | collective-permute-start | bytes 737288 | tf_op jit(solution)/shard_map/ppermute | solution.py:576
  259.4 15.6 %collective-permute-start.5 = (bf16[1,4,240,128]{3,2,1,0:T(8,128)(2,1)}, bf16[1,4,240,128]{3,2,1,0:T(8,128)(2,1)}, u32[]{:S(2)}, u32[]{:S(2)}) collective-permute-start(bf16[1,4,240,128]{3,2,1,0:T(8,128)(2,1)} %collective-permute-done.1.refs_5_), channel_id=1, source_target_pairs={{0,7},{1,0},{2,1},{3,2},{4,3},{5,4},{6,5},{7,6},{8,15},{9,8},{10,9... | collective-permute-start | bytes 737288 | tf_op jit(solution)/shard_map/ppermute | solution.py:576
  271.7 15.6 %collective-permute-start.10 = (bf16[2,4,240,128]{3,2,1,0:T(8,128)(2,1)}, bf16[2,4,240,128]{3,2,1,0:T(8,128)(2,1)}, u32[]{:S(2)}, u32[]{:S(2)}) collective-permute-start(bf16[2,4,240,128]{3,2,1,0:T(8,128)(2,1)} %collective-permute-done.6.refs_2_), channel_id=1, source_target_pairs={{0,1},{1,2},{2,3},{3,4},{4,5},{5,6},{6,7},{7,0},{8,9},{9,10},{10,1... | collective-permute-start | bytes 1474568 | tf_op jit(solution)/shard_map/ppermute | solution.py:576
  275.0 15.7 %collective-permute-start.8 = (bf16[1,4,240,128]{3,2,1,0:T(8,128)(2,1)}, bf16[1,4,240,128]{3,2,1,0:T(8,128)(2,1)}, u32[]{:S(2)}, u32[]{:S(2)}) collective-permute-start(bf16[1,4,240,128]{3,2,1,0:T(8,128)(2,1)} %collective-permute-done.4.refs_4_), channel_id=1, source_target_pairs={{0,1},{1,2},{2,3},{3,4},{4,5},{5,6},{6,7},{7,0},{8,9},{9,10},{10,1... | collective-permute-start | bytes 737288 | tf_op jit(solution)/shard_map/ppermute | solution.py:576
  275.1 15.6 %collective-permute-start.9 = (bf16[1,4,240,128]{3,2,1,0:T(8,128)(2,1)}, bf16[1,4,240,128]{3,2,1,0:T(8,128)(2,1)}, u32[]{:S(2)}, u32[]{:S(2)}) collective-permute-start(bf16[1,4,240,128]{3,2,1,0:T(8,128)(2,1)} %collective-permute-done.5.refs_5_), channel_id=1, source_target_pairs={{0,7},{1,0},{2,1},{3,2},{4,3},{5,4},{6,5},{7,6},{8,15},{9,8},{10,9... | collective-permute-start | bytes 737288 | tf_op jit(solution)/shard_map/ppermute | solution.py:576
  287.4 15.6 %collective-permute-start.14 = (bf16[2,4,240,128]{3,2,1,0:T(8,128)(2,1)}, bf16[2,4,240,128]{3,2,1,0:T(8,128)(2,1)}, u32[]{:S(2)}, u32[]{:S(2)}) collective-permute-start(bf16[2,4,240,128]{3,2,1,0:T(8,128)(2,1)} %collective-permute-done.10.refs_2_), channel_id=1, source_target_pairs={{0,1},{1,2},{2,3},{3,4},{4,5},{5,6},{6,7},{7,0},{8,9},{9,10},{10,1... | collective-permute-start | bytes 1474568 | tf_op jit(solution)/shard_map/ppermute | solution.py:576
  290.7 15.7 %collective-permute-start.12 = (bf16[1,4,240,128]{3,2,1,0:T(8,128)(2,1)}, bf16[1,4,240,128]{3,2,1,0:T(8,128)(2,1)}, u32[]{:S(2)}, u32[]{:S(2)}) collective-permute-start(bf16[1,4,240,128]{3,2,1,0:T(8,128)(2,1)} %collective-permute-done.8.refs_4_), channel_id=1, source_target_pairs={{0,1},{1,2},{2,3},{3,4},{4,5},{5,6},{6,7},{7,0},{8,9},{9,10},{10,1... | collective-permute-start | bytes 737288 | tf_op jit(solution)/shard_map/ppermute | solution.py:576
  290.7 15.6 %collective-permute-start.13 = (bf16[1,4,240,128]{3,2,1,0:T(8,128)(2,1)}, bf16[1,4,240,128]{3,2,1,0:T(8,128)(2,1)}, u32[]{:S(2)}, u32[]{:S(2)}) collective-permute-start(bf16[1,4,240,128]{3,2,1,0:T(8,128)(2,1)} %collective-permute-done.9.refs_5_), channel_id=1, source_target_pairs={{0,7},{1,0},{2,1},{3,2},{4,3},{5,4},{6,5},{7,6},{8,15},{9,8},{10,9... | collective-permute-start | bytes 737288 | tf_op jit(solution)/shard_map/ppermute | solution.py:576
  303.0 15.6 %collective-permute-start.18 = (bf16[2,4,240,128]{3,2,1,0:T(8,128)(2,1)}, bf16[2,4,240,128]{3,2,1,0:T(8,128)(2,1)}, u32[]{:S(2)}, u32[]{:S(2)}) collective-permute-start(bf16[2,4,240,128]{3,2,1,0:T(8,128)(2,1)} %collective-permute-done.14.refs_2_), channel_id=1, source_target_pairs={{0,1},{1,2},{2,3},{3,4},{4,5},{5,6},{6,7},{7,0},{8,9},{9,10},{10,1... | collective-permute-start | bytes 1474568 | tf_op jit(solution)/shard_map/ppermute | solution.py:576
  306.4 15.7 %collective-permute-start.16 = (bf16[1,4,240,128]{3,2,1,0:T(8,128)(2,1)}, bf16[1,4,240,128]{3,2,1,0:T(8,128)(2,1)}, u32[]{:S(2)}, u32[]{:S(2)}) collective-permute-start(bf16[1,4,240,128]{3,2,1,0:T(8,128)(2,1)} %collective-permute-done.12.refs_4_), channel_id=1, source_target_pairs={{0,1},{1,2},{2,3},{3,4},{4,5},{5,6},{6,7},{7,0},{8,9},{9,10},{10,1... | collective-permute-start | bytes 737288 | tf_op jit(solution)/shard_map/ppermute | solution.py:576
  306.4 15.7 %collective-permute-start.17 = (bf16[1,4,240,128]{3,2,1,0:T(8,128)(2,1)}, bf16[1,4,240,128]{3,2,1,0:T(8,128)(2,1)}, u32[]{:S(2)}, u32[]{:S(2)}) collective-permute-start(bf16[1,4,240,128]{3,2,1,0:T(8,128)(2,1)} %collective-permute-done.13.refs_5_), channel_id=1, source_target_pairs={{0,7},{1,0},{2,1},{3,2},{4,3},{5,4},{6,5},{7,6},{8,15},{9,8},{10,9... | collective-permute-start | bytes 737288 | tf_op jit(solution)/shard_map/ppermute | solution.py:576
  318.7 15.7 %collective-permute-start.22 = (bf16[2,4,240,128]{3,2,1,0:T(8,128)(2,1)}, bf16[2,4,240,128]{3,2,1,0:T(8,128)(2,1)}, u32[]{:S(2)}, u32[]{:S(2)}) collective-permute-start(bf16[2,4,240,128]{3,2,1,0:T(8,128)(2,1)} %collective-permute-done.18.refs_2_), channel_id=1, source_target_pairs={{0,1},{1,2},{2,3},{3,4},{4,5},{5,6},{6,7},{7,0},{8,9},{9,10},{10,1... | collective-permute-start | bytes 1474568 | tf_op jit(solution)/shard_map/ppermute | solution.py:576
  318.8 15.6 %collective-permute-start.23 = (bf16[2,4,240,128]{3,2,1,0:T(8,128)(2,1)}, bf16[2,4,240,128]{3,2,1,0:T(8,128)(2,1)}, u32[]{:S(2)}, u32[]{:S(2)}) collective-permute-start(bf16[2,4,240,128]{3,2,1,0:T(8,128)(2,1)} %collective-permute-done.19.refs_3_), channel_id=1, source_target_pairs={{0,7},{1,0},{2,1},{3,2},{4,3},{5,4},{6,5},{7,6},{8,15},{9,8},{10,9... | collective-permute-start | bytes 1474568 | tf_op jit(solution)/shard_map/ppermute | solution.py:576
  322.1 17.1 %collective-permute-start.20 = (bf16[1,4,240,128]{3,2,1,0:T(8,128)(2,1)}, bf16[1,4,240,128]{3,2,1,0:T(8,128)(2,1)}, u32[]{:S(2)}, u32[]{:S(2)}) collective-permute-start(bf16[1,4,240,128]{3,2,1,0:T(8,128)(2,1)} %collective-permute-done.16.refs_4_), channel_id=1, source_target_pairs={{0,1},{1,2},{2,3},{3,4},{4,5},{5,6},{6,7},{7,0},{8,9},{9,10},{10,1... | collective-permute-start | bytes 737288 | tf_op jit(solution)/shard_map/ppermute | solution.py:576
  322.1 17.1 %collective-permute-start.21 = (bf16[1,4,240,128]{3,2,1,0:T(8,128)(2,1)}, bf16[1,4,240,128]{3,2,1,0:T(8,128)(2,1)}, u32[]{:S(2)}, u32[]{:S(2)}) collective-permute-start(bf16[1,4,240,128]{3,2,1,0:T(8,128)(2,1)} %collective-permute-done.17.refs_5_), channel_id=1, source_target_pairs={{0,7},{1,0},{2,1},{3,2},{4,3},{5,4},{6,5},{7,6},{8,15},{9,8},{10,9... | collective-permute-start | bytes 737288 | tf_op jit(solution)/shard_map/ppermute | solution.py:576
  334.4 16.2 %collective-permute-start.26 = (bf16[2,4,240,128]{3,2,1,0:T(8,128)(2,1)}, bf16[2,4,240,128]{3,2,1,0:T(8,128)(2,1)}, u32[]{:S(2)}, u32[]{:S(2)}) collective-permute-start(bf16[2,4,240,128]{3,2,1,0:T(8,128)(2,1)} %collective-permute-done.22.refs_0_), channel_id=1, source_target_pairs={{0,1},{1,2},{2,3},{3,4},{4,5},{5,6},{6,7},{7,0},{8,9},{9,10},{10,1... | collective-permute-start | bytes 1474568 | tf_op jit(solution)/shard_map/ppermute | solution.py:576
  334.5 16.0 %collective-permute-start.27 = (bf16[2,4,240,128]{3,2,1,0:T(8,128)(2,1)}, bf16[2,4,240,128]{3,2,1,0:T(8,128)(2,1)}, u32[]{:S(2)}, u32[]{:S(2)}) collective-permute-start(bf16[2,4,240,128]{3,2,1,0:T(8,128)(2,1)} %collective-permute-done.23.refs_1_), channel_id=1, source_target_pairs={{0,7},{1,0},{2,1},{3,2},{4,3},{5,4},{6,5},{7,6},{8,15},{9,8},{10,9... | collective-permute-start | bytes 1474568 | tf_op jit(solution)/shard_map/ppermute | solution.py:576
  339.2 16.2 %collective-permute-start.24 = (bf16[1,4,240,128]{3,2,1,0:T(8,128)(2,1)}, bf16[1,4,240,128]{3,2,1,0:T(8,128)(2,1)}, u32[]{:S(2)}, u32[]{:S(2)}) collective-permute-start(bf16[1,4,240,128]{3,2,1,0:T(8,128)(2,1)} %collective-permute-done.20.refs_0_), channel_id=1, source_target_pairs={{0,1},{1,2},{2,3},{3,4},{4,5},{5,6},{6,7},{7,0},{8,9},{9,10},{10,1... | collective-permute-start | bytes 737288 | tf_op jit(solution)/shard_map/ppermute | solution.py:576
  339.2 16.2 %collective-permute-start.25 = (bf16[1,4,240,128]{3,2,1,0:T(8,128)(2,1)}, bf16[1,4,240,128]{3,2,1,0:T(8,128)(2,1)}, u32[]{:S(2)}, u32[]{:S(2)}) collective-permute-start(bf16[1,4,240,128]{3,2,1,0:T(8,128)(2,1)} %collective-permute-done.21.refs_1_), channel_id=1, source_target_pairs={{0,7},{1,0},{2,1},{3,2},{4,3},{5,4},{6,5},{7,6},{8,15},{9,8},{10,9... | collective-permute-start | bytes 737288 | tf_op jit(solution)/shard_map/ppermute | solution.py:576
  (4 other events, 62.1 us)

commit v4 on v3

--- a/solution.py
+++ b/solution.py
@@ -47,7 +47,7 @@
 def step_kernel(s, x_hbm, dy_hbm, wg_hbm, wu_hbm, wd_hbm, *refs):
     (near_x, near_y, all_x), refs = (refs[0:2], refs[2:4], refs[4:6]), refs[6:]
     (wg, wu, wd, xh, a, a_t, dh, dh_t, dg, du, hid, own, got, final, gathered, gs, us, ds, hs, ps, first_in, second_in) = refs[:22]
-    (load_sem, w_sem, send_sem, recv_sem, out_sem, gather_send, gather_recv) = refs[22:]
+    (load_sem, w_sem, send_sem, recv_sem), out_sems, (gather_send, gather_recv) = refs[22:26], refs[26:28], refs[28:]
     me = lax.axis_index("dp")
     right, left = lax.rem(me + 1, s.n), lax.rem(me + s.n - 1, s.n)
     towards = (right, left)
@@ -269,8 +269,8 @@
             unit = lax.select(q == start, i, unit)
         return unit
 
+    inner(1, 0, 0)
     finish(blocks - 1, True)
-    inner(1, 0, 0)
     pl.semaphore_wait(barrier, 2)
 
     def period(q, carry):
@@ -315,7 +315,7 @@
             for copy in pieces(0) + pieces(1):
                 copy.start()
 
-        @pl.when(q == late + s.units)
+        @pl.when(q == late + s.units + 2)
         def _():
             for copy in outs(0):
                 copy.start()
@@ -345,19 +345,22 @@
     def outs(last):
         pairs, before = [], s.part - 1
         for way in range(2):
+            x, y, half = near_x[way], near_y[way], s.part // 2
             if last:
                 pairs += [
                     (gathered.at[way, :, before], all_x[way].at[pl.ds(1, s.n - 1), before]),
-                    (final.at[3, way], near_y[way].at[0]),
+                    (final.at[3, way, pl.ds(before, 1)], y.at[pl.ds(before, 1)]),
                 ]
             else:
                 pairs += [
                     (final.at[0, way], all_x[way].at[0]),
                     (gathered.at[way, :, pl.ds(0, before)], all_x[way].at[pl.ds(1, s.n - 1), pl.ds(0, before)]),
-                    (final.at[1, way], near_y[way].at[1]),
-                    (final.at[2, way], near_x[way]),
+                    (final.at[2, way], x.at[pl.ds(0, s.part)]),
+                    (final.at[1, way, pl.ds(0, half)], x.at[pl.ds(s.part, half)]),
+                    (final.at[1, way, pl.ds(half, half)], y.at[pl.ds(s.part, half)]),
+                    (final.at[3, way, pl.ds(0, before)], y.at[pl.ds(0, before)]),
                 ]
-        return [pltpu.make_async_copy(*pair, out_sem.at[last, i]) for i, pair in enumerate(pairs)]
+        return [pltpu.make_async_copy(*pair, out_sems[last].at[i]) for i, pair in enumerate(pairs)]
 
     def pieces(which):
         cols = pl.ds(0, TILE) if which == 0 else pl.ds(TILE, s.ff - TILE)
@@ -376,7 +379,8 @@
 
 def reduced_shards(s, x, dy, w_gate, w_up, w_down):
     part = (s.part, s.message, LANES)
-    shapes = [jax.ShapeDtypeStruct(lead + part, BF16) for lead in ((), (s.layers,), (s.n,)) for _ in range(2)]
+    ring = (s.part + s.part // 2, s.message, LANES)
+    shapes = [jax.ShapeDtypeStruct(shape, BF16) for shape in (ring, ring, (s.n, *part)) for _ in range(2)]
     d, t, ff = s.d, s.tokens, s.ff
     any_space = pl.BlockSpec(memory_space=pl.ANY)
     out = pl.pallas_call(
@@ -411,7 +415,8 @@
             pltpu.SemaphoreType.DMA((3, 2)),
             pltpu.SemaphoreType.DMA((SLOTS, 2)),
             pltpu.SemaphoreType.DMA((SLOTS, 2, s.far)),
-            pltpu.SemaphoreType.DMA((2, 8)),
+            pltpu.SemaphoreType.DMA((12,)),
+            pltpu.SemaphoreType.DMA((4,)),
             pltpu.SemaphoreType.DMA((s.part, 2)),
             pltpu.SemaphoreType.DMA((s.part, s.n - 1, 2)),
         ],
@@ -430,7 +435,7 @@
 AHEAD = 2
 
 
-def adamw_kernel(s, items, operands, *refs):
+def adamw_kernel(s, span, items, operands, *refs):
     messages, refs = refs[: 2 * operands], refs[2 * operands :]
     state, refs = (refs[0:3], refs[3:6], refs[6:9]), refs[9:]
     refs = refs[len(refs) - 24 :]
@@ -450,36 +455,40 @@
         return out
 
     def places(item, way, group):
-        layer, part, away = of(0, item), of(1, item), of(2, item)
+        layer, first, away = of(0, item), of(1, item), of(2, item)
         chunk = lax.rem(me + (s.n - away if way == 0 else away), s.n)
         rows = pl.ds(pl.multiple_of(chunk * s.rows, s.rows), s.rows)
-        cols = pl.ds(pl.multiple_of(part * (s.part * TILE), s.part * TILE), s.part * TILE)
-        units = pl.ds(part * s.part, s.part)
+        cols = pl.ds(pl.multiple_of(first * TILE, span * TILE), span * TILE)
+        units = pl.ds(first, span)
         return [ref.at[layer, rows, cols] for ref in group[way]] + [ref.at[layer, units, way, chunk] for ref in group[2]]
 
     def loads(item, way):
         spots = [ref.at[item, way] for ref in (*across_in, *down_in)]
         return [
-            pltpu.make_async_copy(*pair, sem_in.at[item, way, 1 + i])
+            pltpu.make_async_copy(*pair, sem_in.at[lax.rem(item, AHEAD + 1), way, 2 + i])
             for i, pair in enumerate(zip(places(item, way, state), spots, strict=True))
         ]
 
-    def message_load(item, way, which):
-        return pltpu.make_async_copy(messages[2 * which + way].at[of(4, item)], message_in.at[item, way], sem_in.at[item, way, 0])
+    def message_loads(item, way, act):
+        for number, one in enumerate(items):
+            @pl.when(item == number)
+            def _():
+                at = 0
+                for i, (which, start, count) in enumerate(one[3]):
+                    spot = message_in.at[number, way, pl.ds(at, count)]
+                    act(pltpu.make_async_copy(messages[2 * which + way].at[pl.ds(start, count)], spot, sem_in.at[number % (AHEAD + 1), way, i]))
+                    at += count
 
     def stores(item, way):
         spots = [ref.at[item, way] for ref in (*across_out, *down_out)]
         return [
-            pltpu.make_async_copy(*pair, sem_out.at[item, way, i])
+            pltpu.make_async_copy(*pair, sem_out.at[lax.rem(item, AHEAD), way, i])
             for i, pair in enumerate(zip(spots, places(item, way, outs), strict=True))
         ]
 
     def fetch(item, carry=0):
         for way in range(2):
-            for which in range(operands):
-                @pl.when(of(3, item) == which)
-                def _():
-                    message_load(item, way, which).start()
+            message_loads(item, way, lambda copy: copy.start())
             for copy in loads(item, way):
                 copy.start()
         return carry
@@ -490,7 +499,7 @@
             fetch(item + AHEAD)
 
         for way in range(2):
-            message_load(item, way, 0).wait()
+            message_loads(item, way, lambda copy: copy.wait())
             for copy in loads(item, way):
                 copy.wait()
 
@@ -511,7 +520,13 @@
                         ref[item, way, unit, :, cols] = value
                 return carry
 
-            lax.fori_loop(0, s.part, unit_step, 0)
+            lax.fori_loop(0, span, unit_step, 0)
+
+            @pl.when(item >= AHEAD)
+            def _():
+                for copy in stores(item - AHEAD, way):
+                    copy.wait()
+
             for copy in stores(item, way):
                 copy.start()
         return carry
@@ -523,12 +538,12 @@
         return carry
 
     for item in range(min(AHEAD, len(items))):
-        fetch(item)
+        fetch(jnp.int32(item))
     lax.fori_loop(0, len(items), work, 0)
-    lax.fori_loop(0, len(items), drain, 0)
-
-
-def adamw_on(s, items, messages, state, so_far):
+    lax.fori_loop(max(len(items) - AHEAD, 0), len(items), drain, 0)
+
+
+def adamw_on(s, span, items, messages, state, so_far):
     flat = [one for group in state for one in group]
     shapes = [jax.ShapeDtypeStruct(one.shape, one.dtype) for one in flat]
     args = [one for pair in messages for one in pair] + flat
@@ -537,22 +552,22 @@
         aliases = {len(args) + i: i for i in range(9)}
         args += so_far
     count = (len(items), 2)
-    across, down = (*count, s.rows, s.part * TILE), (*count, s.part, s.down, s.d)
+    across, down = (*count, s.rows, span * TILE), (*count, span, s.down, s.d)
     types = (BF16, F32, F32)
     buffers = [pltpu.VMEM(shape, dtype) for shape in (across, down) for dtype in types]
-    numbers = 2 * len(items) * s.part * s.message * LANES
+    numbers = 2 * len(items) * span * s.message * LANES
     any_space = pl.BlockSpec(memory_space=pl.ANY)
     return list(
         pl.pallas_call(
-            functools.partial(adamw_kernel, s, items, len(messages)),
+            functools.partial(adamw_kernel, s, span, items, len(messages)),
             out_shape=shapes,
             in_specs=[any_space] * len(args),
             out_specs=[any_space] * 9,
             input_output_aliases=aliases,
-            scratch_shapes=[pltpu.VMEM((*count, s.part, s.message, LANES), BF16)]
+            scratch_shapes=[pltpu.VMEM((*count, span, s.message, LANES), BF16)]
             + buffers
             + buffers
-            + [pltpu.SemaphoreType.DMA((*count, 7)), pltpu.SemaphoreType.DMA((*count, 6))],
+            + [pltpu.SemaphoreType.DMA((AHEAD + 1, 2, 8)), pltpu.SemaphoreType.DMA((AHEAD, 2, 6))],
             compiler_params=pltpu.CompilerParams(vmem_limit_bytes=67043328),
             cost_estimate=pl.CostEstimate(flops=numbers * 20 * 1000, bytes_accessed=numbers * 22, transcendentals=numbers),
         )(*args)
@@ -566,7 +581,7 @@
         weights, m, v = (arrays[i : i + 3] for i in (0, 3, 6))
         s = Sizes(mesh, x, weights[0])
         near_x, near_y, all_x = reduced_shards(s, x, dy, *weights)
-        near_x = [one[None] for one in near_x]
+        all_x = [one.reshape(n * s.part, s.message, LANES) for one in all_x]
         by_chunk = (s.layers, s.units, 2, s.n, s.down, s.d)
         state = [list(group) for group in zip(weights, m, v, strict=True)]
         state[2] = [one.reshape(by_chunk) for one in state[2]]
@@ -576,22 +591,24 @@
             return [lax.ppermute(one, "dp", ring) for one, ring in zip(pair, rings, strict=True)]
 
         out, now_x, now_y = None, near_x, near_y
+        part, half = s.part, s.part // 2
         for hop in range(n):
             this_x, this_y = now_x, now_y
-            y_items = [(0, 1, hop, 1, 0), (1, 1, hop, 1, 1)]
             if hop < n - 1:
                 if hop > 0:
                     this_y, _ = lax.optimization_barrier((this_y, before))
                     this_x, _ = lax.optimization_barrier((this_x, this_y))
                 before = this_x
                 now_y, now_x = shift(this_y), shift(this_x)
-            here = [(1, 0, away, 0, away) for away in (range(3) if hop == 0 else [hop + 2] if hop + 2 < n else [])]
-            if here:
-                out = adamw_on(s, [*here, *y_items, (0, 0, hop, 2, 0)], [all_x, this_y, this_x], state, out)
+                early = range(2) if hop == 0 else [hop + 1]
+                items = [(1, 0, away, ((2, away * part, part),)) for away in early]
+                items += [(0, part, hop, ((1, 0, part),)), (1, part, hop, ((0, part, half), (1, part, half))), (0, 0, hop, ((0, 0, part),))]
+                out = adamw_on(s, part, items, [this_x, this_y, all_x], state, out)
             else:
-                y_items = [(layer, part, away, 0, place) for layer, part, away, _, place in y_items]
-                out = adamw_on(s, y_items, [this_y], state, out)
-                out = adamw_on(s, [(0, 0, hop, 0, 0)], [this_x], state, out)
+                for messages, first in ((this_y, part), (this_x, 0)):
+                    items = [(0, first + i, hop, ((0, i, half),)) for i in range(0, part, half)]
+                    items += [(1, part + (half if first else 0), hop, ((0, part, half),))]
+                    out = adamw_on(s, half, items, [messages], state, out)
         out[6:9] = [one.reshape(weights[2].shape) for one in out[6:9]]
         return tuple(out[3 * which + i] for i in range(3) for which in range(3))
 

time: 359 us -> 357 us (level)
    pallas_call x10 -> x9, Pallas kernels: 74.5 us -> 71.5 us  [adamw_on(): pl.pallas_call(functools.partial(adamw_kernel, s, span, items, len(messag...]
  transfers between devices with their start and end apart: 28 -> 28, of which waited for: 2 -> 3; matrix products, arithmetic and copies ran while one was open for 0% -> 0% of each run, Pallas kernels for 20% -> 19%
where the time goes in v4:
time: 357 us
  Pallas kernels  307 us (86%)
  starting transfers between devices  45.9 us (13%)
    pallas_call x1, Pallas kernels, reduced_shards(): pl.pallas_call(functools.partial(step_kernel, s), out_shape=shapes, in_sp...  236 us
    pallas_call x9, Pallas kernels, adamw_on(): pl.pallas_call(functools.partial(adamw_kernel, s, span, items, len(messag...  71.5 us
    ppermute x28, starting transfers between devices, shift(): lax.ppermute(one, 'dp', ring)  45.9 us
  transfers between devices with their start and end apart: 28, of which 3 were waited for; matrix products, arithmetic and copies ran while one was open for 0% of the time, Pallas kernels for 19%

profile of v4, /device:TPU:22, one launch (start us, length us, event | category | flops | bytes accessed | tf_op | source)
XLA Modules:
  0.0 356.8 jit_solution(3686362263302876988)
XLA Ops:
  0.6 235.7 %shard_map.178 = (bf16[6,240,128]{2,1,0:T(8,128)(2,1)}, bf16[6,240,128]{2,1,0:T(8,128)(2,1)}, bf16[6,240,128]{2,1,0:T(8,128)(2,1)}, bf16[6,240,128]{2,1,0:T(8,12...) custom-call(bf16[1,2048,640]{2,1,0:T(8,128)(2,1)} %x_hbm.1, bf16[1,2048,640]{2,1,0:T(8,128)(2,1)} %dy_hbm.1, ...), custom_call_target="tpu_custom_call" | custom-call | tf_op jit(solution)/shard_map/pallas_call | solution.py:386
  236.4 3.2 collective-permute-start.3
  239.7 3.2 collective-permute-start.1
  242.9 10.9 %shard_map.179 = (bf16[2,640,2048]{2,1,0:T(8,128)(2,1)}, f32[2,640,2048]{2,1,0:T(8,128)}, f32[2,640,2048]{2,1,0:T(8,128)}, bf16[2,640,2048]{2,1,0:T(8,128)(2,1)}...) custom-call(bf16[6,240,128]{2,1,0:T(8,128)(2,1)} %get-tuple-element., ...), custom_call_target="tpu_custom_call" | custom-call | flops 24576000000 | bytes 27033600 | tf_op jit(solution)/shard_map/pallas_call | solution.py:561
  253.9 3.2 collective-permute-start.7
  257.1 3.2 collective-permute-start.5
  260.3 8.7 %shard_map.180 = (bf16[2,640,2048]{2,1,0:T(8,128)(2,1)}, f32[2,640,2048]{2,1,0:T(8,128)}, f32[2,640,2048]{2,1,0:T(8,128)}, bf16[2,640,2048]{2,1,0:T(8,128)(2,1)}...) custom-call(bf16[6,240,128]{2,1,0:T(8,128)(2,1)} %collective-permute, ...), custom_call_target="tpu_custom_call", output_to_operand_aliasing={{0}: (15, {}), {1}: (16, {}), {2}: (17, {}), {3}: (18, {}),... | custom-call | flops 19660800000 | bytes 21626880 | tf_op jit(solution)/shard_map/pallas_call | solution.py:561
  269.2 3.2 collective-permute-start.11
  272.5 3.2 collective-permute-start.9
  275.7 8.7 %shard_map.181 = (bf16[2,640,2048]{2,1,0:T(8,128)(2,1)}, f32[2,640,2048]{2,1,0:T(8,128)}, f32[2,640,2048]{2,1,0:T(8,128)}, bf16[2,640,2048]{2,1,0:T(8,128)(2,1)}...) custom-call(bf16[6,240,128]{2,1,0:T(8,128)(2,1)} %collective-permute, ...), custom_call_target="tpu_custom_call", output_to_operand_aliasing={{0}: (15, {}), {1}: (16, {}), {2}: (17, {}), {3}: (18, {}),... | custom-call | flops 19660800000 | bytes 21626880 | tf_op jit(solution)/shard_map/pallas_call | solution.py:561
  284.6 3.2 collective-permute-start.15
  287.8 3.2 collective-permute-start.13
  291.1 8.7 %shard_map.182 = (bf16[2,640,2048]{2,1,0:T(8,128)(2,1)}, f32[2,640,2048]{2,1,0:T(8,128)}, f32[2,640,2048]{2,1,0:T(8,128)}, bf16[2,640,2048]{2,1,0:T(8,128)(2,1)}...) custom-call(bf16[6,240,128]{2,1,0:T(8,128)(2,1)} %collective-permute, ...), custom_call_target="tpu_custom_call", output_to_operand_aliasing={{0}: (15, {}), {1}: (16, {}), {2}: (17, {}), {3}: (18, {}),... | custom-call | flops 19660800000 | bytes 21626880 | tf_op jit(solution)/shard_map/pallas_call | solution.py:561
  300.0 3.2 collective-permute-start.19
  303.7 3.2 collective-permute-start.17
  307.0 8.7 %shard_map.183 = (bf16[2,640,2048]{2,1,0:T(8,128)(2,1)}, f32[2,640,2048]{2,1,0:T(8,128)}, f32[2,640,2048]{2,1,0:T(8,128)}, bf16[2,640,2048]{2,1,0:T(8,128)(2,1)}...) custom-call(bf16[6,240,128]{2,1,0:T(8,128)(2,1)} %collective-permute, ...), custom_call_target="tpu_custom_call", output_to_operand_aliasing={{0}: (15, {}), {1}: (16, {}), {2}: (17, {}), {3}: (18, {}),... | custom-call | flops 19660800000 | bytes 21626880 | tf_op jit(solution)/shard_map/pallas_call | solution.py:561
  315.9 3.2 collective-permute-start.23
  320.5 3.2 collective-permute-start.21
  323.7 8.7 %shard_map.184 = (bf16[2,640,2048]{2,1,0:T(8,128)(2,1)}, f32[2,640,2048]{2,1,0:T(8,128)}, f32[2,640,2048]{2,1,0:T(8,128)}, bf16[2,640,2048]{2,1,0:T(8,128)(2,1)}...) custom-call(bf16[6,240,128]{2,1,0:T(8,128)(2,1)} %collective-permute, ...), custom_call_target="tpu_custom_call", output_to_operand_aliasing={{0}: (15, {}), {1}: (16, {}), {2}: (17, {}), {3}: (18, {}),... | custom-call | flops 19660800000 | bytes 21626880 | tf_op jit(solution)/shard_map/pallas_call | solution.py:561
  332.6 3.2 collective-permute-start.27
  336.4 3.2 collective-permute-start.25
  339.6 8.7 %shard_map.185 = (bf16[2,640,2048]{2,1,0:T(8,128)(2,1)}, f32[2,640,2048]{2,1,0:T(8,128)}, f32[2,640,2048]{2,1,0:T(8,128)}, bf16[2,640,2048]{2,1,0:T(8,128)(2,1)}...) custom-call(bf16[6,240,128]{2,1,0:T(8,128)(2,1)} %collective-permute, ...), custom_call_target="tpu_custom_call", output_to_operand_aliasing={{0}: (15, {}), {1}: (16, {}), {2}: (17, {}), {3}: (18, {}),... | custom-call | flops 19660800000 | bytes 21626880 | tf_op jit(solution)/shard_map/pallas_call | solution.py:561
  348.4 4.1 %shard_map.186 = (bf16[2,640,2048]{2,1,0:T(8,128)(2,1)}, f32[2,640,2048]{2,1,0:T(8,128)}, f32[2,640,2048]{2,1,0:T(8,128)}, bf16[2,640,2048]{2,1,0:T(8,128)(2,1)}...) custom-call(bf16[6,240,128]{2,1,0:T(8,128)(2,1)} %collective-permute, ...), custom_call_target="tpu_custom_call", output_to_operand_aliasing={{0}: (11, {}), {1}: (12, {}), {2}: (13, {}), {3}: (14, {}),... | custom-call | flops 7372800000 | bytes 8110080 | tf_op jit(solution)/shard_map/pallas_call | solution.py:561
  352.5 4.1 %shard_map.187 = (bf16[2,640,2048]{2,1,0:T(8,128)(2,1)}, f32[2,640,2048]{2,1,0:T(8,128)}, f32[2,640,2048]{2,1,0:T(8,128)}, bf16[2,640,2048]{2,1,0:T(8,128)(2,1)}...) custom-call(bf16[6,240,128]{2,1,0:T(8,128)(2,1)} %collective-permute, ...), custom_call_target="tpu_custom_call", output_to_operand_aliasing={{0}: (11, {}), {1}: (12, {}), {2}: (13, {}), {3}: (14, {}),... | custom-call | flops 7372800000 | bytes 8110080 | tf_op jit(solution)/shard_map/pallas_call | solution.py:561
  (42 shorter events, 3.5 us)
Async XLA Ops:
  236.3 17.4 %collective-permute-start.2 = (bf16[6,240,128]{2,1,0:T(8,128)(2,1)}, bf16[6,240,128]{2,1,0:T(8,128)(2,1)}, u32[]{:S(2)}, u32[]{:S(2)}) collective-permute-start(bf16[6,240,128]{2,1,0:T(8,128)(2,1)} %get-tuple-element.122.refs_2_), channel_id=1, source_target_pairs={{0,1},{1,2},{2,3},{3,4},{4,5},{5,6},{6,7},{7,0},{8,9},{9,10},{10,1... | collective-permute-start | bytes 1105928 | tf_op jit(solution)/shard_map/ppermute | solution.py:591
  236.4 17.3 %collective-permute-start.3 = (bf16[6,240,128]{2,1,0:T(8,128)(2,1)}, bf16[6,240,128]{2,1,0:T(8,128)(2,1)}, u32[]{:S(2)}, u32[]{:S(2)}) collective-permute-start(bf16[6,240,128]{2,1,0:T(8,128)(2,1)} %get-tuple-element.123.refs_3_), channel_id=1, source_target_pairs={{0,7},{1,0},{2,1},{3,2},{4,3},{5,4},{6,5},{7,6},{8,15},{9,8},{10,9... | collective-permute-start | bytes 1105928 | tf_op jit(solution)/shard_map/ppermute | solution.py:591
  239.6 17.5 %collective-permute-start = (bf16[6,240,128]{2,1,0:T(8,128)(2,1)}, bf16[6,240,128]{2,1,0:T(8,128)(2,1)}, u32[]{:S(2)}, u32[]{:S(2)}) collective-permute-start(bf16[6,240,128]{2,1,0:T(8,128)(2,1)} %get-tuple-element.120.refs_0_), channel_id=1, source_target_pairs={{0,1},{1,2},{2,3},{3,4},{4,5},{5,6},{6,7},{7,0},{8,9},{9,10},{10,1... | collective-permute-start | bytes 1105928 | tf_op jit(solution)/shard_map/ppermute | solution.py:591
  239.7 17.5 %collective-permute-start.1 = (bf16[6,240,128]{2,1,0:T(8,128)(2,1)}, bf16[6,240,128]{2,1,0:T(8,128)(2,1)}, u32[]{:S(2)}, u32[]{:S(2)}) collective-permute-start(bf16[6,240,128]{2,1,0:T(8,128)(2,1)} %get-tuple-element.121.refs_1_), channel_id=1, source_target_pairs={{0,7},{1,0},{2,1},{3,2},{4,3},{5,4},{6,5},{7,6},{8,15},{9,8},{10,9... | collective-permute-start | bytes 1105928 | tf_op jit(solution)/shard_map/ppermute | solution.py:591
  253.8 15.3 %collective-permute-start.6 = (bf16[6,240,128]{2,1,0:T(8,128)(2,1)}, bf16[6,240,128]{2,1,0:T(8,128)(2,1)}, u32[]{:S(2)}, u32[]{:S(2)}) collective-permute-start(bf16[6,240,128]{2,1,0:T(8,128)(2,1)} %collective-permute-done.2.refs_2_), channel_id=1, source_target_pairs={{0,1},{1,2},{2,3},{3,4},{4,5},{5,6},{6,7},{7,0},{8,9},{9,10},{10,1... | collective-permute-start | bytes 1105928 | tf_op jit(solution)/shard_map/ppermute | solution.py:591
  257.1 15.4 %collective-permute-start.4 = (bf16[6,240,128]{2,1,0:T(8,128)(2,1)}, bf16[6,240,128]{2,1,0:T(8,128)(2,1)}, u32[]{:S(2)}, u32[]{:S(2)}) collective-permute-start(bf16[6,240,128]{2,1,0:T(8,128)(2,1)} %collective-permute-done.refs_0_), channel_id=1, source_target_pairs={{0,1},{1,2},{2,3},{3,4},{4,5},{5,6},{6,7},{7,0},{8,9},{9,10},{10,1... | collective-permute-start | bytes 1105928 | tf_op jit(solution)/shard_map/ppermute | solution.py:591
  257.1 15.3 %collective-permute-start.5 = (bf16[6,240,128]{2,1,0:T(8,128)(2,1)}, bf16[6,240,128]{2,1,0:T(8,128)(2,1)}, u32[]{:S(2)}, u32[]{:S(2)}) collective-permute-start(bf16[6,240,128]{2,1,0:T(8,128)(2,1)} %collective-permute-done.1.refs_1_), channel_id=1, source_target_pairs={{0,7},{1,0},{2,1},{3,2},{4,3},{5,4},{6,5},{7,6},{8,15},{9,8},{10,9... | collective-permute-start | bytes 1105928 | tf_op jit(solution)/shard_map/ppermute | solution.py:591
  269.1 15.3 %collective-permute-start.10 = (bf16[6,240,128]{2,1,0:T(8,128)(2,1)}, bf16[6,240,128]{2,1,0:T(8,128)(2,1)}, u32[]{:S(2)}, u32[]{:S(2)}) collective-permute-start(bf16[6,240,128]{2,1,0:T(8,128)(2,1)} %collective-permute-done.6.refs_2_), channel_id=1, source_target_pairs={{0,1},{1,2},{2,3},{3,4},{4,5},{5,6},{6,7},{7,0},{8,9},{9,10},{10,1... | collective-permute-start | bytes 1105928 | tf_op jit(solution)/shard_map/ppermute | solution.py:591
  272.5 15.3 %collective-permute-start.8 = (bf16[6,240,128]{2,1,0:T(8,128)(2,1)}, bf16[6,240,128]{2,1,0:T(8,128)(2,1)}, u32[]{:S(2)}, u32[]{:S(2)}) collective-permute-start(bf16[6,240,128]{2,1,0:T(8,128)(2,1)} %collective-permute-done.4.refs_0_), channel_id=1, source_target_pairs={{0,1},{1,2},{2,3},{3,4},{4,5},{5,6},{6,7},{7,0},{8,9},{9,10},{10,1... | collective-permute-start | bytes 1105928 | tf_op jit(solution)/shard_map/ppermute | solution.py:591
  284.5 15.3 %collective-permute-start.14 = (bf16[6,240,128]{2,1,0:T(8,128)(2,1)}, bf16[6,240,128]{2,1,0:T(8,128)(2,1)}, u32[]{:S(2)}, u32[]{:S(2)}) collective-permute-start(bf16[6,240,128]{2,1,0:T(8,128)(2,1)} %collective-permute-done.10.refs_2_), channel_id=1, source_target_pairs={{0,1},{1,2},{2,3},{3,4},{4,5},{5,6},{6,7},{7,0},{8,9},{9,10},{10,1... | collective-permute-start | bytes 1105928 | tf_op jit(solution)/shard_map/ppermute | solution.py:591
  287.8 15.9 %collective-permute-start.12 = (bf16[6,240,128]{2,1,0:T(8,128)(2,1)}, bf16[6,240,128]{2,1,0:T(8,128)(2,1)}, u32[]{:S(2)}, u32[]{:S(2)}) collective-permute-start(bf16[6,240,128]{2,1,0:T(8,128)(2,1)} %collective-permute-done.8.refs_0_), channel_id=1, source_target_pairs={{0,1},{1,2},{2,3},{3,4},{4,5},{5,6},{6,7},{7,0},{8,9},{9,10},{10,1... | collective-permute-start | bytes 1105928 | tf_op jit(solution)/shard_map/ppermute | solution.py:591
  287.8 15.9 %collective-permute-start.13 = (bf16[6,240,128]{2,1,0:T(8,128)(2,1)}, bf16[6,240,128]{2,1,0:T(8,128)(2,1)}, u32[]{:S(2)}, u32[]{:S(2)}) collective-permute-start(bf16[6,240,128]{2,1,0:T(8,128)(2,1)} %collective-permute-done.9.refs_1_), channel_id=1, source_target_pairs={{0,7},{1,0},{2,1},{3,2},{4,3},{5,4},{6,5},{7,6},{8,15},{9,8},{10,9... | collective-permute-start | bytes 1105928 | tf_op jit(solution)/shard_map/ppermute | solution.py:591
  299.8 15.9 %collective-permute-start.18 = (bf16[6,240,128]{2,1,0:T(8,128)(2,1)}, bf16[6,240,128]{2,1,0:T(8,128)(2,1)}, u32[]{:S(2)}, u32[]{:S(2)}) collective-permute-start(bf16[6,240,128]{2,1,0:T(8,128)(2,1)} %collective-permute-done.14.refs_2_), channel_id=1, source_target_pairs={{0,1},{1,2},{2,3},{3,4},{4,5},{5,6},{6,7},{7,0},{8,9},{9,10},{10,1... | collective-permute-start | bytes 1105928 | tf_op jit(solution)/shard_map/ppermute | solution.py:591
  300.0 15.8 %collective-permute-start.19 = (bf16[6,240,128]{2,1,0:T(8,128)(2,1)}, bf16[6,240,128]{2,1,0:T(8,128)(2,1)}, u32[]{:S(2)}, u32[]{:S(2)}) collective-permute-start(bf16[6,240,128]{2,1,0:T(8,128)(2,1)} %collective-permute-done.15.refs_3_), channel_id=1, source_target_pairs={{0,7},{1,0},{2,1},{3,2},{4,3},{5,4},{6,5},{7,6},{8,15},{9,8},{10,9... | collective-permute-start | bytes 1105928 | tf_op jit(solution)/shard_map/ppermute | solution.py:591
  303.7 16.8 %collective-permute-start.16 = (bf16[6,240,128]{2,1,0:T(8,128)(2,1)}, bf16[6,240,128]{2,1,0:T(8,128)(2,1)}, u32[]{:S(2)}, u32[]{:S(2)}) collective-permute-start(bf16[6,240,128]{2,1,0:T(8,128)(2,1)} %collective-permute-done.12.refs_0_), channel_id=1, source_target_pairs={{0,1},{1,2},{2,3},{3,4},{4,5},{5,6},{6,7},{7,0},{8,9},{9,10},{10,1... | collective-permute-start | bytes 1105928 | tf_op jit(solution)/shard_map/ppermute | solution.py:591
  303.7 16.8 %collective-permute-start.17 = (bf16[6,240,128]{2,1,0:T(8,128)(2,1)}, bf16[6,240,128]{2,1,0:T(8,128)(2,1)}, u32[]{:S(2)}, u32[]{:S(2)}) collective-permute-start(bf16[6,240,128]{2,1,0:T(8,128)(2,1)} %collective-permute-done.13.refs_1_), channel_id=1, source_target_pairs={{0,7},{1,0},{2,1},{3,2},{4,3},{5,4},{6,5},{7,6},{8,15},{9,8},{10,9... | collective-permute-start | bytes 1105928 | tf_op jit(solution)/shard_map/ppermute | solution.py:591
  315.7 16.8 %collective-permute-start.22 = (bf16[6,240,128]{2,1,0:T(8,128)(2,1)}, bf16[6,240,128]{2,1,0:T(8,128)(2,1)}, u32[]{:S(2)}, u32[]{:S(2)}) collective-permute-start(bf16[6,240,128]{2,1,0:T(8,128)(2,1)} %collective-permute-done.18.refs_2_), channel_id=1, source_target_pairs={{0,1},{1,2},{2,3},{3,4},{4,5},{5,6},{6,7},{7,0},{8,9},{9,10},{10,1... | collective-permute-start | bytes 1105928 | tf_op jit(solution)/shard_map/ppermute | solution.py:591
  315.9 16.7 %collective-permute-start.23 = (bf16[6,240,128]{2,1,0:T(8,128)(2,1)}, bf16[6,240,128]{2,1,0:T(8,128)(2,1)}, u32[]{:S(2)}, u32[]{:S(2)}) collective-permute-start(bf16[6,240,128]{2,1,0:T(8,128)(2,1)} %collective-permute-done.19.refs_3_), channel_id=1, source_target_pairs={{0,7},{1,0},{2,1},{3,2},{4,3},{5,4},{6,5},{7,6},{8,15},{9,8},{10,9... | collective-permute-start | bytes 1105928 | tf_op jit(solution)/shard_map/ppermute | solution.py:591
  320.5 15.9 %collective-permute-start.20 = (bf16[6,240,128]{2,1,0:T(8,128)(2,1)}, bf16[6,240,128]{2,1,0:T(8,128)(2,1)}, u32[]{:S(2)}, u32[]{:S(2)}) collective-permute-start(bf16[6,240,128]{2,1,0:T(8,128)(2,1)} %collective-permute-done.16.refs_0_), channel_id=1, source_target_pairs={{0,1},{1,2},{2,3},{3,4},{4,5},{5,6},{6,7},{7,0},{8,9},{9,10},{10,1... | collective-permute-start | bytes 1105928 | tf_op jit(solution)/shard_map/ppermute | solution.py:591
  320.5 15.9 %collective-permute-start.21 = (bf16[6,240,128]{2,1,0:T(8,128)(2,1)}, bf16[6,240,128]{2,1,0:T(8,128)(2,1)}, u32[]{:S(2)}, u32[]{:S(2)}) collective-permute-start(bf16[6,240,128]{2,1,0:T(8,128)(2,1)} %collective-permute-done.17.refs_1_), channel_id=1, source_target_pairs={{0,7},{1,0},{2,1},{3,2},{4,3},{5,4},{6,5},{7,6},{8,15},{9,8},{10,9... | collective-permute-start | bytes 1105928 | tf_op jit(solution)/shard_map/ppermute | solution.py:591
  332.5 15.9 %collective-permute-start.26 = (bf16[6,240,128]{2,1,0:T(8,128)(2,1)}, bf16[6,240,128]{2,1,0:T(8,128)(2,1)}, u32[]{:S(2)}, u32[]{:S(2)}) collective-permute-start(bf16[6,240,128]{2,1,0:T(8,128)(2,1)} %collective-permute-done.22.refs_2_), channel_id=1, source_target_pairs={{0,1},{1,2},{2,3},{3,4},{4,5},{5,6},{6,7},{7,0},{8,9},{9,10},{10,1... | collective-permute-start | bytes 1105928 | tf_op jit(solution)/shard_map/ppermute | solution.py:591
  332.6 15.8 %collective-permute-start.27 = (bf16[6,240,128]{2,1,0:T(8,128)(2,1)}, bf16[6,240,128]{2,1,0:T(8,128)(2,1)}, u32[]{:S(2)}, u32[]{:S(2)}) collective-permute-start(bf16[6,240,128]{2,1,0:T(8,128)(2,1)} %collective-permute-done.23.refs_3_), channel_id=1, source_target_pairs={{0,7},{1,0},{2,1},{3,2},{4,3},{5,4},{6,5},{7,6},{8,15},{9,8},{10,9... | collective-permute-start | bytes 1105928 | tf_op jit(solution)/shard_map/ppermute | solution.py:591
  336.4 16.1 %collective-permute-start.24 = (bf16[6,240,128]{2,1,0:T(8,128)(2,1)}, bf16[6,240,128]{2,1,0:T(8,128)(2,1)}, u32[]{:S(2)}, u32[]{:S(2)}) collective-permute-start(bf16[6,240,128]{2,1,0:T(8,128)(2,1)} %collective-permute-done.20.refs_0_), channel_id=1, source_target_pairs={{0,1},{1,2},{2,3},{3,4},{4,5},{5,6},{6,7},{7,0},{8,9},{9,10},{10,1... | collective-permute-start | bytes 1105928 | tf_op jit(solution)/shard_map/ppermute | solution.py:591
  336.4 16.1 %collective-permute-start.25 = (bf16[6,240,128]{2,1,0:T(8,128)(2,1)}, bf16[6,240,128]{2,1,0:T(8,128)(2,1)}, u32[]{:S(2)}, u32[]{:S(2)}) collective-permute-start(bf16[6,240,128]{2,1,0:T(8,128)(2,1)} %collective-permute-done.21.refs_1_), channel_id=1, source_target_pairs={{0,7},{1,0},{2,1},{3,2},{4,3},{5,4},{6,5},{7,6},{8,15},{9,8},{10,9... | collective-permute-start | bytes 1105928 | tf_op jit(solution)/shard_map/ppermute | solution.py:591
  (4 other events, 61.0 us)
